TPU v7x, 32 devices: a whole 2x2x4 slice. The times are simulated.
32 devices in a mesh: groups: 2 (over y), tensor: 4 (over z), seq: 2 (over x), section: 2 (over core).
Axes of the slice: x: 2, y: 2, z: 4, core: 2. Of those that a mesh axis runs over, the one named last changes fastest.
Arguments:
- attn_out: bfloat16 [768, 8192], P(('groups', 'seq'), ('tensor', 'section')), parts along dimension 0, may hold values from -6 to 6
- residual: bfloat16 [768, 8192], P(('groups', 'seq'), ('tensor', 'section')), parts along dimension 0, may hold values from -120 to 120
- out_weight: bfloat16 [8192, 8192], P(('tensor', 'section')), may hold values from -0.09375 to 0.09375
- norm_gain: bfloat16 [8192], replicated, may hold values from 0.099609375 to 1.8984375
- gate_up: bfloat16 [8192, 2, 16384], P(None, None, ('tensor', 'seq', 'section')), may hold values from -0.0625 to 0.0625
Outputs:
- stream: bfloat16 [768, 8192], P(('groups', 'seq'), ('tensor', 'section')), parts along dimension 0
- hidden: bfloat16 [768, 16384], P('groups', ('tensor', 'seq', 'section')), parts along dimension 0
There are 2 independent parts, one for each index of `groups`. A program takes and returns all parts, laid end to end along the dimension named above; an argument that names none is the same for every part. Nothing has to cross between parts.
All inputs are finite; a program needn't handle non-finite values.
Results may differ from a plain program's by a relative error of at most 0.012.
Values may be sent and summed in bfloat16 or wider, within the bound.
No kernel may reach another device: no remote copies, remote signals or barrier semaphores. Data moves between devices by JAX's collectives and lax.ppermute only.
A program may use at most 192 MiB of HBM per device.

v0:
```python
import jax
import jax.numpy as jnp
from jax import lax
from jax.sharding import PartitionSpec as P

D = 8192


epsilon = 1e-06


def partner(x, axis, distance):
    return lax.ppermute(x, axis, [(i, i ^ 1 << distance) for i in range(lax.axis_size(axis))])


def local(attn_out, residual, out_weight, norm_gain, gate_up):
    axis_size = lax.axis_size(("tensor", "section"))
    position = lax.axis_index(("tensor", "section"))
    row_count, shard_width = attn_out.shape
    partial_value = jnp.dot(attn_out, out_weight, preferred_element_type=jnp.float32).astype(
        jnp.bfloat16
    )
    blocked = partial_value.reshape(row_count, axis_size, shard_width)
    for level_index in range(axis_size.bit_length() - 1):
        paired = blocked.reshape(row_count, blocked.shape[1] // 2, 2, shard_width)
        my_bit = position >> level_index & 1
        kept_half = lax.dynamic_index_in_dim(paired, my_bit, 2, keepdims=False)
        sent_half = lax.dynamic_index_in_dim(paired, 1 - my_bit, 2, keepdims=False)
        received = partner(sent_half, ("tensor", "section"), level_index)
        blocked = (kept_half.astype(jnp.float32) + received.astype(jnp.float32)).astype(
            jnp.bfloat16
        )
    projected = blocked.reshape(row_count, shard_width)
    stream = (projected.astype(jnp.float32) + residual.astype(jnp.float32)).astype(jnp.bfloat16)
    full_stream = lax.all_gather(stream, ("tensor", "section"), axis=1, tiled=True).astype(
        jnp.float32
    )
    totals = jnp.sum(full_stream * full_stream, axis=1, keepdims=True)
    normed_rows = (
        full_stream * lax.rsqrt(totals / D + epsilon) * norm_gain.astype(jnp.float32)
    ).astype(jnp.bfloat16)
    hidden_cols = gate_up.shape[2]
    local_weight = gate_up.reshape(D, 2 * hidden_cols)
    row_block = lax.all_gather(normed_rows, "seq", axis=0, tiled=True)
    products = jnp.dot(row_block, local_weight, preferred_element_type=jnp.float32)
    products = products.reshape(row_block.shape[0], 2, hidden_cols)
    hidden = (jax.nn.silu(products[:, 0]) * products[:, 1]).astype(jnp.bfloat16)
    return (stream, hidden)


def solution(mesh):
    placed = (
        P(("groups", "seq"), ("tensor", "section")),
        P(("groups", "seq"), ("tensor", "section")),
        P(("tensor", "section"), None),
        P(),
        P(None, None, ("tensor", "seq", "section")),
    )
    return jax.shard_map(
        local,
        mesh=mesh,
        in_specs=placed,
        out_specs=(
            P(("groups", "seq"), ("tensor", "section")),
            P("groups", ("tensor", "seq", "section")),
        ),
        check_vma=False,
    )
```

profile of v0, /device:TPU:15, one launch (start us, length us, event | category | flops | bytes accessed | tf_op | source)
XLA Modules:
  0.0 235.6 jit_solution(17975186885308728960)
XLA Ops:
  7.2 0.0 copy-start
  7.2 0.0 all-gather.3.cloned.1.call-start
  7.2 0.9 copy-done
  8.2 10.8 %convolution_convert_fusion = bf16[192,8192]{1,0:T(8,128)(2,1)} fusion(bf16[192,1024]{1,0:T(8,128)(2,1)S(1)} %copy-done, bf16[1024,8192]{1,0:T(8,128)(2,1)} %param.7), kind=kOutput, calls=%fused_computation | convolution fusion | flops 3222798336 | bytes 20316160 | tf_op jit(solution)/shard_map/dot_general | solution.py:20
  19.0 4.9 %reshape_reshape.3 = bf16[192,4,2,1024]{3,2,1,0:T(2,128)(2,1)S(1)} reshape(bf16[192,8192]{1,0:T(8,128)(2,1)} %convolution_convert_fusion) | data formatting | bytes 6291456 | tf_op jit(solution)/shard_map/reshape;reshape | solution.py:25
  23.9 8.4 %constant_dynamic-slice_fusion.2 = (bf16[192,4,1,1024]{3,2,1,0:T(2,128)(2,1)}, bf16[192,4,1,1024]{3,2,1,0:T(2,128)(2,1)S(1)}) fusion(bf16[192,4,2,1024]{3,2,1,0:T(2,128)(2,1)S(1)} %reshape_reshape.3, s32[]{:T(128)S(6)} %select_n.21, s32[]{:T(128)S(6)} %select_n.22), kind=kLoop, calls=%fused_computation.25 | loop fusion | bytes 6291464 | tf_op jit(solution)/shard_map/jit(dynamic_index_in_dim)/dynamic_slice | solution.py:27
  32.3 0.0 copy-start.2
  32.3 2.9 %copy.20 = bf16[192,4,1,1024]{3,0,2,1:T(8,128)(2,1)} copy(bf16[192,4,1,1024]{3,2,1,0:T(2,128)(2,1)S(1)} %get-tuple-element.3) | data formatting | bytes 3145728
  35.2 0.7 collective-permute-start
  35.8 3.4 %collective-permute-done = bf16[192,4,1024]{2,0,1:T(8,128)(2,1)} collective-permute-done((bf16[192,4,1024]{2,0,1:T(8,128)(2,1)}, bf16[192,4,1024]{2,0,1:T(8,128)(2,1)}, u32[]{:S(2)}, u32[]{:S(2)}) %collective-permute-start) | collective-permute-done | bytes 1572896 | tf_op jit(solution)/shard_map/ppermute | solution.py:13
  39.2 0.0 copy-done.2
  39.2 3.2 %fusion.5 = bf16[192,4,1024]{2,0,1:T(8,128)(2,1)S(1)} fusion(bf16[192,4,1024]{2,0,1:T(8,128)(2,1)} %collective-permute-done, bf16[192,4,1,1024]{3,2,1,0:T(2,128)(2,1)S(1)} %copy-done.2), kind=kLoop, calls=%fused_computation.9 | loop fusion | flops 3145728 | bytes 4718592 | tf_op jit(solution)/shard_map/convert_element_type | solution.py:30
  42.4 0.0 copy-start.4
  42.5 0.0 copy-start.5
  42.5 1.1 copy-done.4
  43.6 0.0 copy-start.6
  43.6 0.1 dynamic-slice_bitcast_fusion
  43.7 0.2 collective-permute-start.1
  43.9 18.6 %collective-permute-done.1 = bf16[192,2,1024]{2,0,1:T(8,128)(2,1)S(1)} collective-permute-done((bf16[192,2,1024]{2,0,1:T(8,128)(2,1)S(1)}, bf16[192,2,1024]{2,0,1:T(8,128)(2,1)S(1)}, u32[]{:S(2)}, u32[]{:S(2)}) %collective-permute-start.1) | collective-permute-done | bytes 786464 | tf_op jit(solution)/shard_map/ppermute | solution.py:13
  62.5 1.4 fusion.8
  64.0 2.4 %collective-permute-start.2 = (bf16[192,1,1024]{2,0,1:T(8,128)(2,1)S(1)}, bf16[192,1,1024]{2,0,1:T(8,128)(2,1)S(1)}, u32[]{:S(2)}, u32[]{:S(2)}) collective-permute-start(bf16[192,1,1024]{2,0,1:T(8,128)(2,1)S(1)} %constant_dynamic-slice_fusion), channel_id=1, source_target_pairs={{0,8},{1,9},{4,12},{5,13},{8,0},{9,1},{12,4},{13,5},{2,10},{3,11},... | collective-permute-start | bytes 1179656 | tf_op jit(solution)/shard_map/ppermute | solution.py:13
  66.3 17.2 %collective-permute-done.2 = bf16[192,1,1024]{2,0,1:T(8,128)(2,1)S(1)} collective-permute-done((bf16[192,1,1024]{2,0,1:T(8,128)(2,1)S(1)}, bf16[192,1,1024]{2,0,1:T(8,128)(2,1)S(1)}, u32[]{:S(2)}, u32[]{:S(2)}) %collective-permute-start.2) | collective-permute-done | bytes 393248 | tf_op jit(solution)/shard_map/ppermute | solution.py:13
  83.5 0.0 copy-done.5
  83.5 0.9 fusion.9
  84.4 0.0 all-gather.3.cloned.1.call-update
  84.5 0.3 all-gather.5.cloned.1.call-start
  84.7 0.0 copy-done.6
  84.7 39.3 %all-gather.3.cloned.1.call-done = bf16[192,8192]{1,0:T(8,128)(2,1)} async-done(((bf16[192,1024]{1,0:T(8,128)(2,1)}), bf16[192,8192]{1,0:T(8,128)(2,1)}) %all-gather.3.cloned.1.call-update) | async-done | bytes 3145744 | tf_op jit(solution)/shard_map/all_gather | solution.py:35
  124.1 0.0 copy-start.3
  124.1 2.8 %fusion = f32[192]{0:T(256)S(1)} fusion(bf16[192,8192]{1,0:T(8,128)(2,1)} %all-gather.3.cloned.1.call-done), kind=kLoop, calls=%fused_computation.3 | loop fusion | flops 4718400 | bytes 3146496 | tf_op jit(solution)/shard_map/reduce_sum | solution.py:38
  126.8 0.1 copy-done.3
  126.9 2.6 %fusion.2 = bf16[192,8192]{1,0:T(8,128)(2,1)} fusion(bf16[192,8192]{1,0:T(8,128)(2,1)S(1)} %copy-done.3, f32[8192]{0:T(1024)S(1)} %convert_element_type.79, f32[192]{0:T(256)S(1)} %add_rsqrt_fusion), kind=kLoop, calls=%fused_computation.5 | loop fusion | flops 6291456 | bytes 6324992 | tf_op jit(solution)/shard_map/convert_element_type | solution.py:41
  129.5 0.0 all-gather.5.cloned.1.call-update
  129.5 24.6 %copy.15 = bf16[1024,8,2,1024]{3,1,2,0:T(8,128)(2,1)} copy(bf16[1024,8,2,1024]{3,2,1,0:T(2,128)(2,1)} %bitcast.43) | data formatting | bytes 67108864
  154.1 40.6 %copy.11 = bf16[2048,8192]{1,0:T(8,128)(2,1)} copy(bf16[2048,8192]{0,1:T(8,128)(2,1)} %bitcast.42) | data formatting | bytes 67108864 | tf_op jit(solution)/shard_map/dot_general | solution.py:45
  194.7 13.6 %all-gather.5.cloned.1.call-done = bf16[384,8192]{1,0:T(8,128)(2,1)} async-done(((bf16[192,8192]{1,0:T(8,128)(2,1)}), bf16[384,8192]{1,0:T(8,128)(2,1)}) %all-gather.5.cloned.1.call-update) | async-done | bytes 6291472 | tf_op jit(solution)/shard_map/all_gather | solution.py:44
  208.3 0.0 copy-start.1
  208.3 19.1 %fusion.3 = f32[384,2,1024]{2,0,1:T(8,128)S(1)} fusion(bf16[2,1024,8192]{2,1,0:T(8,128)(2,1)} %bitcast.44, bf16[384,8192]{1,0:T(8,128)(2,1)} %all-gather.5.cloned.1.call-done), kind=kOutput, calls=%fused_computation.6 | convolution fusion | flops 12884901888 | bytes 42991616 | tf_op jit(solution)/shard_map/dot_general | solution.py:45
  227.4 1.4 fusion.7
  228.7 0.0 copy-done.1
  (3 shorter events, 0.1 us)
Async XLA Ops:
  7.2 1.0 copy-start
  7.2 116.9 %all-gather.3.cloned.1.call-start = ((), (), s32[]{:S(2)}) async-start(), calls=%async_computation | async-start | bytes 3538944 | tf_op jit(solution)/shard_map/all_gather | solution.py:35
  32.3 6.9 %copy-start.2 = (bf16[192,4,1,1024]{3,2,1,0:T(2,128)(2,1)S(1)}, bf16[192,4,1,1024]{3,2,1,0:T(2,128)(2,1)}, u32[]{:S(2)}) copy-start(bf16[192,4,1,1024]{3,2,1,0:T(2,128)(2,1)} %get-tuple-element.2) | copy-start | bytes 4718596
  35.2 4.1 %collective-permute-start = (bf16[192,4,1024]{2,0,1:T(8,128)(2,1)}, bf16[192,4,1024]{2,0,1:T(8,128)(2,1)}, u32[]{:S(2)}, u32[]{:S(2)}) collective-permute-start(bf16[192,4,1024]{2,0,1:T(8,128)(2,1)} %bitcast.41), channel_id=1, source_target_pairs={{0,1},{1,0},{4,5},{5,4},{8,9},{9,8},{12,13},{13,12},{2,3},{3,2},{6... | collective-permute-start | bytes 4718600 | tf_op jit(solution)/shard_map/ppermute | solution.py:13
  42.4 1.2 copy-start.4
  42.5 41.0 %copy-start.5 = (bf16[192,1024]{1,0:T(8,128)(2,1)S(1)}, bf16[192,1024]{1,0:T(8,128)(2,1)}, u32[]{:S(2)}) copy-start(bf16[192,1024]{1,0:T(8,128)(2,1)} %param.6) | copy-start | bytes 1179652
  43.6 41.1 %copy-start.6 = (bf16[8192]{0:T(1024)(128)(2,1)S(1)}, bf16[8192]{0:T(1024)(128)(2,1)}, u32[]{:S(2)}) copy-start(bf16[8192]{0:T(1024)(128)(2,1)} %param.8) | copy-start | bytes 49156
  43.7 18.8 %collective-permute-start.1 = (bf16[192,2,1024]{2,0,1:T(8,128)(2,1)S(1)}, bf16[192,2,1024]{2,0,1:T(8,128)(2,1)S(1)}, u32[]{:S(2)}, u32[]{:S(2)}) collective-permute-start(bf16[192,2,1024]{2,0,1:T(8,128)(2,1)S(1)} %dynamic-slice_bitcast_fusion), channel_id=1, source_target_pairs={{0,4},{1,5},{4,0},{5,1},{8,12},{9,13},{12,8},{13,9},{2,6},{3,7},{6... | collective-permute-start | bytes 2359304 | tf_op jit(solution)/shard_map/ppermute | solution.py:13
  64.0 19.5 %collective-permute-start.2 = (bf16[192,1,1024]{2,0,1:T(8,128)(2,1)S(1)}, bf16[192,1,1024]{2,0,1:T(8,128)(2,1)S(1)}, u32[]{:S(2)}, u32[]{:S(2)}) collective-permute-start(bf16[192,1,1024]{2,0,1:T(8,128)(2,1)S(1)} %constant_dynamic-slice_fusion), channel_id=1, source_target_pairs={{0,8},{1,9},{4,12},{5,13},{8,0},{9,1},{12,4},{13,5},{2,10},{3,11},... | collective-permute-start | bytes 1179656 | tf_op jit(solution)/shard_map/ppermute | solution.py:13
  84.5 123.8 %all-gather.5.cloned.1.call-start = ((), (), s32[]{:S(2)}) async-start(), calls=%async_computation.1 | async-start | bytes 9437184 | tf_op jit(solution)/shard_map/all_gather | solution.py:44
  124.1 2.8 %copy-start.3 = (bf16[192,8192]{1,0:T(8,128)(2,1)S(1)}, bf16[192,8192]{1,0:T(8,128)(2,1)}, u32[]{:S(2)}) copy-start(bf16[192,8192]{1,0:T(8,128)(2,1)} %all-gather.3.cloned.1.call-done) | copy-start | bytes 9437188
  208.3 20.5 %copy-start.1 = (bf16[192,1024]{1,0:T(8,128)(2,1)S(1)}, bf16[192,1024]{1,0:T(8,128)(2,1)}, u32[]{:S(2)}) copy-start(bf16[192,1024]{1,0:T(8,128)(2,1)} %param.5) | copy-start | bytes 1179652
Sparse Core Ops, SparseCore 0:
  84.6 39.4 all-gather.2
  129.6 78.6 all-gather.4
where the time goes:
time: 240 us; the launch traced here: 236 us
  waiting for transfers between devices  92.1 us (38%)
  local copies, waits for them, and re-layouts  83.6 us (35%)
  matrix products  29.9 us (12%)
  between operations  14.1 us (6%)
  other arithmetic  12.3 us (5%)
  starting transfers between devices  3.58 us (1%)
    dot_general x1, local copies, waits for them, and re-layouts, local(): jnp.dot(row_block, local_weight, preferred_element_type=jnp.float32)  40.6 us
    all_gather x1, waiting for transfers between devices, local(): lax.all_gather(stream, ('tensor', 'section'), axis=1, tiled=True)  39.3 us
    ppermute x3, waiting for transfers between devices, partner(): lax.ppermute(x, axis, [(i, i ^ 1 << distance) for i in range(lax.axis_siz...  39.1 us
    unnamed x16, local copies, waits for them, and re-layouts  29.6 us
    dot_general x1, matrix products, local(): jnp.dot(row_block, local_weight, preferred_element_type=jnp.float32)  19.1 us
    all_gather x1, waiting for transfers between devices, local(): row_block = lax.all_gather(normed_rows, 'seq', axis=0, tiled=True)  13.6 us
    dot_general x1, matrix products, local(): jnp.dot(attn_out, out_weight, preferred_element_type=jnp.float32)  10.8 us
    dynamic_slice x1, local copies, waits for them, and re-layouts, local(): kept_half = lax.dynamic_index_in_dim(paired, my_bit, 2, keepdims=False)  8.36 us
  transfers between devices with their start and end apart: 5, of which 5 were waited for; matrix products, arithmetic and copies ran while one was open for 28% of the time, Pallas kernels for 0%

commit v1 on v0

v1 whole, which is shorter than its diff:
```python
import math

import jax
import jax.numpy as jnp
from jax import lax
from jax.experimental import pallas as pl
from jax.experimental.pallas import tpu as pltpu
from jax.sharding import PartitionSpec as P

EPSILON = 1e-06
BF16 = jnp.bfloat16
F32 = jnp.float32
LINE = ("tensor", "section")
RELAYOUT_CALLS = 4
LONGEST_LINE = 8


def tile_of(size, limit):
    return math.gcd(size, limit)


def project(scalars, attn_out, out_weight, width):
    rows, depth = attn_out.shape
    tile = tile_of(width, 512)
    tiles = width // tile

    def weight_at(j, t, s):
        first = jnp.where(s[2] > 0, s[0] * tiles + t, jnp.where(s[3] > 0, s[1] * tiles, 0))
        second = jnp.where(s[3] > 0, s[1] * tiles + t, jnp.where(s[2] > 0, (s[0] + 1) * tiles - 1, 0))
        return 0, jnp.where(j == 0, first, second)

    def body(s, x_ref, w_ref, keep_ref, send_ref):
        @pl.when((pl.program_id(0) == 0) & (s[2] > 0))
        def _():
            keep_ref[...] = jnp.dot(x_ref[...], w_ref[...], preferred_element_type=F32).astype(BF16)

        @pl.when((pl.program_id(0) == 1) & (s[3] > 0))
        def _():
            send_ref[...] = jnp.dot(x_ref[...], w_ref[...], preferred_element_type=F32).astype(BF16)

    return pl.pallas_call(
        body,
        grid_spec=pltpu.PrefetchScalarGridSpec(
            num_scalar_prefetch=1,
            grid=(2, tiles),
            in_specs=[
                pl.BlockSpec((rows, depth), lambda j, t, s: (0, 0)),
                pl.BlockSpec((depth, tile), weight_at),
            ],
            out_specs=[
                pl.BlockSpec((rows, tile), lambda j, t, s: (0, jnp.where(j == 0, t, tiles - 1))),
                pl.BlockSpec((rows, tile), lambda j, t, s: (0, jnp.where(j == 0, 0, t))),
            ],
        ),
        out_shape=[jax.ShapeDtypeStruct((rows, width), BF16)] * 2,
        compiler_params=pltpu.CompilerParams(vmem_limit_bytes=12 << 20),
        name="project",
    )(scalars, attn_out, out_weight)


def split_weight(gate_up, buffer, call, calls):
    depth, _, cols = gate_up.shape
    span = depth // calls
    tile = tile_of(span, 256)
    steps = span // tile

    def body(w_ref, *refs):
        refs[-1][...] = jnp.swapaxes(w_ref[...], 0, 1)

    operands = [gate_up]
    in_specs = [pl.BlockSpec((tile, 2, cols), lambda i: (call * steps + i, 0, 0))]
    aliases = {}
    if buffer is not None:
        operands.append(buffer)
        in_specs.append(pl.BlockSpec(memory_space=pl.ANY))
        aliases = {1: 0}
    return pl.pallas_call(
        body,
        grid=(steps,),
        in_specs=in_specs,
        out_specs=pl.BlockSpec((2, tile, cols), lambda i: (0, call * steps + i, 0)),
        out_shape=jax.ShapeDtypeStruct((2, depth, cols), BF16),
        input_output_aliases=aliases,
        compiler_params=pltpu.CompilerParams(vmem_limit_bytes=12 << 20),
        name="split_weight",
    )(*operands)


def gate_products(scalars, blocks, gain, weight, carry, final):
    chunks = len(blocks[0])
    rows, width = blocks[0][0].shape
    _, depth, cols = weight.shape
    tile = tile_of(width, 512)
    tiles = width // tile
    total = chunks * rows
    sides = len(blocks)

    def block_at(j, t, s):
        index = s[0] * tiles + t
        for side in range(sides - 1, -1, -1):
            others = [k for k in range(sides) if k != side]
            here = s[side] * tiles + t
            if others:
                other = others[0]
                stay = s[other] * tiles + (0 if side == 0 else tiles - 1)
                here = jnp.where(s[2 + side] > 0, here, jnp.where(s[2 + other] > 0, stay, 0))
            index = here if side == sides - 1 else jnp.where(j == side, here, index)
        return index

    def chunk_spec(side):
        def at(j, t, s):
            return 0, jnp.where(j == side, t, 0 if side else tiles - 1)

        return pl.BlockSpec((rows, tile), at)

    first = carry is None

    def body(s, *refs):
        refs = list(refs)
        x_refs = [[refs.pop(0) for _ in range(chunks)] for _ in range(sides)]
        gain_ref, w_ref = refs.pop(0), refs.pop(0)
        if not first:
            acc_in, sq_in = refs.pop(0), refs.pop(0)
        if final:
            out_ref, staged, acc, squares = refs
        else:
            acc, squares, staged = refs
        j, t = pl.program_id(0), pl.program_id(1)

        @pl.when((j == 0) & (t == 0))
        def _():
            if first:
                acc[...] = jnp.zeros_like(acc)
                squares[...] = jnp.zeros_like(squares)
            else:
                acc[...] = acc_in[...]
                squares[...] = sq_in[...]

        for side in range(sides):

            @pl.when((j == side) & (s[2 + side] > 0))
            def _():
                for chunk in range(chunks):
                    x = x_refs[side][chunk][...].astype(F32)
                    at = pl.ds(chunk * rows, rows)
                    squares[at, :] += jnp.sum(x * x, axis=1, keepdims=True)
                    staged[at, :] = (x * gain_ref[...]).astype(BF16)
                for half in range(2):
                    acc[half] += jnp.dot(staged[...], w_ref[half], preferred_element_type=F32)

        if final:

            @pl.when((j == sides - 1) & (t == tiles - 1))
            def _():
                for chunk in range(chunks):
                    at = pl.ds(chunk * rows, rows)
                    scale = lax.rsqrt(squares[at, :] / depth + EPSILON)
                    gate = acc[0, at, :] * scale
                    up = acc[1, at, :] * scale
                    out_ref[pl.ds(s[4 + chunk] * rows, rows), :] = (gate / (1.0 + jnp.exp(-gate)) * up).astype(BF16)

    acc_shape, sq_shape = (2, total, cols), (total, 1)
    operands = [*blocks[0]] + ([*blocks[1]] if sides > 1 else []) + [gain, weight]
    in_specs = [chunk_spec(side) for side in range(sides) for _ in range(chunks)] + [
        pl.BlockSpec((1, tile), lambda j, t, s: (0, block_at(j, t, s))),
        pl.BlockSpec((2, tile, cols), lambda j, t, s: (0, block_at(j, t, s), 0)),
    ]
    acc_spec = pl.BlockSpec(acc_shape, lambda j, t, s: (0, 0, 0))
    sq_spec = pl.BlockSpec(sq_shape, lambda j, t, s: (0, 0))
    aliases = {}
    if not first:
        if not final:
            aliases = {1 + len(operands): 0, 2 + len(operands): 1}
        operands += list(carry)
        in_specs += [acc_spec, sq_spec]
    scratch = [pltpu.VMEM((total, tile), BF16)]
    if final:
        out_shape = jax.ShapeDtypeStruct((total, cols), BF16)
        out_specs = pl.BlockSpec((total, cols), lambda j, t, s: (0, 0))
        scratch += [pltpu.VMEM(acc_shape, F32), pltpu.VMEM(sq_shape, F32)]
    else:
        out_shape = [jax.ShapeDtypeStruct(acc_shape, F32), jax.ShapeDtypeStruct(sq_shape, F32)]
        out_specs = [acc_spec, sq_spec]
    return pl.pallas_call(
        body,
        grid_spec=pltpu.PrefetchScalarGridSpec(
            num_scalar_prefetch=1, grid=(sides, tiles), in_specs=in_specs, out_specs=out_specs, scratch_shapes=scratch
        ),
        out_shape=out_shape,
        input_output_aliases=aliases,
        compiler_params=pltpu.CompilerParams(vmem_limit_bytes=32 << 20),
        name="gate_products",
    )(scalars, *operands)


def swap_cores(x):
    return lax.ppermute(x, "section", [(0, 1), (1, 0)])


def scalar_row(*values):
    return jnp.stack([jnp.asarray(v, jnp.int32) for v in values])


def long_line(attn_out, residual, out_weight, norm_gain, gate_up):
    size, position = lax.axis_size(LINE), lax.axis_index(LINE)
    row_count, shard = attn_out.shape
    blocked = jnp.dot(attn_out, out_weight, preferred_element_type=F32).astype(BF16).reshape(row_count, size, shard)
    for level in range(size.bit_length() - 1):
        paired = blocked.reshape(row_count, blocked.shape[1] // 2, 2, shard)
        bit = position >> level & 1
        kept = lax.dynamic_index_in_dim(paired, bit, 2, keepdims=False)
        sent = lax.dynamic_index_in_dim(paired, 1 - bit, 2, keepdims=False)
        received = lax.ppermute(sent, LINE, [(i, i ^ 1 << level) for i in range(size)])
        blocked = (kept.astype(F32) + received.astype(F32)).astype(BF16)
    stream = (blocked.reshape(row_count, shard).astype(F32) + residual.astype(F32)).astype(BF16)
    wide = lax.all_gather(stream, LINE, axis=1, tiled=True).astype(F32)
    depth, _, cols = gate_up.shape
    mean_square = jnp.sum(wide * wide, axis=1, keepdims=True) / depth
    normed = (wide * lax.rsqrt(mean_square + EPSILON) * norm_gain.astype(F32)).astype(BF16)
    normed = lax.all_gather(normed, "seq", axis=0, tiled=True)
    products = jnp.dot(normed, gate_up.reshape(depth, 2 * cols), preferred_element_type=F32)
    products = products.reshape(normed.shape[0], 2, cols)
    return stream, (jax.nn.silu(products[:, 0]) * products[:, 1]).astype(BF16)


def local(attn_out, residual, out_weight, norm_gain, gate_up):
    if lax.axis_size("tensor") > LONGEST_LINE:
        return long_line(attn_out, residual, out_weight, norm_gain, gate_up)
    line, cores, replicas = (lax.axis_size(name) for name in ("tensor", "section", "seq"))
    z, core, x = (lax.axis_index(name) for name in ("tensor", "section", "seq"))
    rows, shard = attn_out.shape
    width = shard * cores
    upward = core == 0

    def add(*terms):
        return sum(term.astype(F32) for term in terms).astype(BF16)

    received = None
    for r in range(1, line):
        up_block, down_block = (z - r) % line, (z + r) % line
        up_valid = (z <= r - 1).astype(jnp.int32)
        down_valid = (z >= line - r).astype(jnp.int32)
        keep_block, send_block = jnp.where(upward, up_block, down_block), jnp.where(upward, down_block, up_block)
        keep_valid, send_valid = jnp.where(upward, up_valid, down_valid), jnp.where(upward, down_valid, up_valid)
        keep, send = project(scalar_row(keep_block, send_block, keep_valid, send_valid), attn_out, out_weight, width)
        to_sibling = [(2 * k + 1, 2 * k) for k in range(r)] + [(2 * k, 2 * k + 1) for k in range(line - r, line)]
        other = lax.ppermute(send, LINE, to_sibling)
        terms = [keep, other] + ([received] if received is not None else [])
        pairs = [(2 * k, 2 * k + 2) for k in range(r)] + [(2 * k + 1, 2 * k - 1) for k in range(line - r, line)]
        received = lax.ppermute(add(*terms), LINE, pairs)
    own, _ = project(scalar_row(z, 0, 1, 0), attn_out, out_weight, width)
    total = add(own, received)
    mine = lax.dynamic_slice_in_dim(total, core * shard, shard, axis=1)
    theirs = swap_cores(lax.dynamic_slice_in_dim(total, (1 - core) * shard, shard, axis=1))
    stream = add(mine, theirs, residual)

    weight = None
    for call in range(RELAYOUT_CALLS):
        weight = split_weight(gate_up, weight, call, RELAYOUT_CALLS)
    gain = norm_gain.astype(F32).reshape(1, -1)

    def pair(a):
        b = swap_cores(a)
        return jnp.where(upward, jnp.concatenate([a, b], axis=1), jnp.concatenate([b, a], axis=1))

    def across(a, senders):
        out = []
        for shift in range(1, replicas):
            pairs = []
            for device in senders:
                for k in range(replicas):
                    there = (k + shift) % replicas
                    k_at, c_at = divmod(device, cores)
                    pairs.append(((k_at * replicas + k) * cores + c_at, (k_at * replicas + there) * cores + c_at))
            out.append(lax.ppermute(a, ("tensor", "seq", "section"), pairs))
        return out

    places = [(x - shift) % replicas for shift in range(replicas)]
    block = pair(stream)
    crossed = [pair(a) for a in across(stream, range(line * cores))]
    carry = gate_products(scalar_row(z, 0, 1, 0, *places), [[block, *crossed]], gain, weight, None, line == 1)
    moving = block
    for r in range(1, line):
        pairs = [(2 * k, 2 * k + 2) for k in range(r - 1, line - 1)]
        pairs += [(2 * k + 1, 2 * k - 1) for k in range(1, line - r + 1)]
        moving = lax.ppermute(moving, LINE, pairs)
        holders = [2 * k for k in range(r, line)] + [2 * k + 1 for k in range(0, line - r)]
        crossed = across(moving, holders)
        chunks = [moving, *crossed]
        others = [swap_cores(a) for a in chunks]
        below, above = z - r, z + r
        here, there = jnp.where(upward, below, above), jnp.where(upward, above, below)
        valid = [((b >= 0) & (b < line)).astype(jnp.int32) for b in (here, there)]
        scalars = scalar_row(here % line, there % line, *valid, *places)
        carry = gate_products(scalars, [chunks, others], gain, weight, carry, r == line - 1)
    return stream, carry


def solution(mesh):
    placed = (
        P(("groups", "seq"), ("tensor", "section")),
        P(("groups", "seq"), ("tensor", "section")),
        P(("tensor", "section"), None),
        P(),
        P(None, None, ("tensor", "seq", "section")),
    )
    return jax.shard_map(
        local,
        mesh=mesh,
        in_specs=placed,
        out_specs=(
            P(("groups", "seq"), ("tensor", "section")),
            P("groups", ("tensor", "seq", "section")),
        ),
        check_vma=False,
    )
```

time: 240 us -> 219 us (0.912); the launches traced: 236 us -> 218 us
  Pallas kernels: 0 us -> 77.5 us
  local copies, waits for them, and re-layouts: 83.6 us -> 36.4 us
  matrix products: 29.9 us -> 0 us
  waiting for transfers between devices: 92.1 us -> 67.4 us
  starting transfers between devices: 3.58 us -> 28.1 us
  between operations: 14.1 us -> 1.21 us
  other arithmetic: 12.3 us -> 6.88 us
    pallas_call x0 -> x12, Pallas kernels: none -> 77.5 us  [the longest x4 38.2 us: gate_products(): pl.pallas_call(body, grid_spec=pltpu.PrefetchScalarGridSpec(num_scalar_pr...]
    all_gather x2 -> x0, waiting for transfers between devices: 52.9 us -> none  [the longest x1 39.3 us: local(): lax.all_gather(stream, ('tensor', 'section'), axis=1, tiled=True)]
    dot_general x1 -> x0, local copies, waits for them, and re-layouts: 40.6 us -> none  [local(): jnp.dot(row_block, local_weight, preferred_element_type=jnp.float32)]
    dot_general x2 -> x0, matrix products: 29.9 us -> none  [the longest x1 19.1 us: local(): jnp.dot(row_block, local_weight, preferred_element_type=jnp.float32)]
    ppermute x3 -> x22, waiting for transfers between devices: 39.1 us -> 67.4 us  [the longest x4 25.5 us: across(): out.append(lax.ppermute(a, ('tensor', 'seq', 'section'), pairs))]
    ppermute x3 -> x22, starting transfers between devices: 3.28 us -> 28.1 us  [the longest x4 7.16 us: across(): out.append(lax.ppermute(a, ('tensor', 'seq', 'section'), pairs))]
    dynamic_slice x1, local copies, waits for them, and re-layouts: 8.36 us -> 0.04 us  [local(): lax.dynamic_slice_in_dim(total, (1 - core) * shard, shard, axis=1)]
    unnamed x16 -> x28, local copies, waits for them, and re-layouts: 29.6 us -> 36 us
  transfers between devices with their start and end apart: 5 -> 22, of which waited for: 5 -> 10; matrix products, arithmetic and copies ran while one was open for 28% -> 3% of each run, Pallas kernels for 0% -> 32%
where the time goes in v1:
time: 219 us; the launch traced here: 218 us
  Pallas kernels  77.5 us (35%)
  waiting for transfers between devices  67.4 us (31%)
  local copies, waits for them, and re-layouts  36.4 us (17%)
  starting transfers between devices  28.1 us (13%)
  other arithmetic  6.88 us (3%)
    pallas_call x4, Pallas kernels, gate_products(): pl.pallas_call(body, grid_spec=pltpu.PrefetchScalarGridSpec(num_scalar_pr...  38.2 us
    unnamed x28, local copies, waits for them, and re-layouts  36 us
    pallas_call x4, Pallas kernels, split_weight(): pl.pallas_call(body, grid=(steps,), in_specs=in_specs, out_specs=pl.Block...  26 us
    ppermute x4, waiting for transfers between devices, across(): out.append(lax.ppermute(a, ('tensor', 'seq', 'section'), pairs))  25.5 us
    ppermute x3, waiting for transfers between devices, local(): moving = lax.ppermute(moving, LINE, pairs)  25.1 us
    pallas_call x4, Pallas kernels, project(): pl.pallas_call(body, grid_spec=pltpu.PrefetchScalarGridSpec(num_scalar_pr...  13.3 us
    ppermute x3, waiting for transfers between devices, local(): received = lax.ppermute(add(*terms), LINE, pairs)  12.8 us
    ppermute x4, starting transfers between devices, across(): out.append(lax.ppermute(a, ('tensor', 'seq', 'section'), pairs))  7.16 us
  transfers between devices with their start and end apart: 22, of which 10 were waited for; matrix products, arithmetic and copies ran while one was open for 3% of the time, Pallas kernels for 32%

profile of v1, /device:TPU:15, one launch (start us, length us, event | category | flops | bytes accessed | tf_op | source)
XLA Modules:
  0.0 217.5 jit_solution(16552983081966393145)
XLA Ops:
  0.8 5.8 %copy-done.1 = bf16[1024,8192]{1,0:T(8,128)(2,1)S(1)} copy-done((bf16[1024,8192]{1,0:T(8,128)(2,1)S(1)}, bf16[1024,8192]{1,0:T(8,128)(2,1)}, u32[]{:S(2)}) %copy-start.1) | copy-done | bytes 16777240
  6.5 1.0 copy-done.5
  7.5 1.3 project.7
  8.8 1.6 collective-permute-start.2
  10.5 5.8 %copy-done.2 = bf16[1024,8192]{1,0:T(8,128)(2,1)S(1)} copy-done((bf16[1024,8192]{1,0:T(8,128)(2,1)S(1)}, bf16[1024,8192]{1,0:T(8,128)(2,1)}, u32[]{:S(2)}) %copy-start.2) | copy-done | bytes 16777240
  16.2 3.0 %project.6 = (bf16[192,2048]{1,0:T(8,128)(2,1)S(1)}, bf16[192,2048]{1,0:T(8,128)(2,1)S(1)}) custom-call(s32[4]{0:T(128)S(1)} %pad_add_fusion.2.s, bf16[192,1024]{1,0:T(8,128)(2,1)S(1)} %copy-done.6, bf16[1024,8192]{1,0:T(8,128)(2,1)S(1)} %copy-done.2), custom_call_target="tpu_custom_call" | custom-call | tf_op jit(solution)/shard_map/project/pallas_call | solution.py:41
  19.3 3.5 %collective-permute-start.1 = (bf16[192,2048]{1,0:T(8,128)(2,1)S(1)}, bf16[192,2048]{1,0:T(8,128)(2,1)}, u32[]{:S(2)}, u32[]{:S(2)}) collective-permute-start(bf16[192,2048]{1,0:T(8,128)(2,1)S(1)} %get-tuple-element.19), channel_id=1, source_target_pairs={{1,0},{5,4},{8,9},{12,13},{3,2},{7,6},{10,11},{14,15},{17,16},{21,... | collective-permute-start | bytes 2359304 | tf_op jit(solution)/shard_map/ppermute | solution.py:247
  22.8 2.3 %add_convert_fusion.3 = bf16[192,2048]{1,0:T(8,128)(2,1)} fusion(bf16[192,2048]{1,0:T(8,128)(2,1)} %collective-permute-done.2, bf16[192,2048]{1,0:T(8,128)(2,1)S(1)} %get-tuple-element.20), kind=kLoop, calls=%fused_computation.3 | loop fusion | flops 1572864 | bytes 2359296 | tf_op jit(solution)/shard_map/convert_element_type | solution.py:236
  25.0 0.7 collective-permute-start.3
  25.9 5.8 %copy-done.3 = bf16[1024,8192]{1,0:T(8,128)(2,1)S(1)} copy-done((bf16[1024,8192]{1,0:T(8,128)(2,1)S(1)}, bf16[1024,8192]{1,0:T(8,128)(2,1)}, u32[]{:S(2)}) %copy-start.3) | copy-done | bytes 16777240
  31.6 4.8 %project.5 = (bf16[192,2048]{1,0:T(8,128)(2,1)S(1)}, bf16[192,2048]{1,0:T(8,128)(2,1)S(1)}) custom-call(s32[4]{0:T(128)S(1)} %pad_add_fusion.1.s, bf16[192,1024]{1,0:T(8,128)(2,1)S(1)} %copy-done.6, bf16[1024,8192]{1,0:T(8,128)(2,1)S(1)} %copy-done.3), custom_call_target="tpu_custom_call" | custom-call | tf_op jit(solution)/shard_map/project/pallas_call | solution.py:41
  36.5 1.9 collective-permute-start
  38.4 1.5 add_convert_fusion.2
  40.0 1.3 collective-permute-start.4
  41.3 11.7 %collective-permute-done.4 = bf16[192,2048]{1,0:T(8,128)(2,1)S(1)} collective-permute-done((bf16[192,2048]{1,0:T(8,128)(2,1)S(1)}, bf16[192,2048]{1,0:T(8,128)(2,1)S(1)}, u32[]{:S(2)}, u32[]{:S(2)}) %collective-permute-start.4) | collective-permute-done | bytes 786464 | tf_op jit(solution)/shard_map/ppermute | solution.py:250
  53.4 1.9 collective-permute-start.5
  55.4 5.8 %copy-done.4 = bf16[1024,8192]{1,0:T(8,128)(2,1)S(1)} copy-done((bf16[1024,8192]{1,0:T(8,128)(2,1)S(1)}, bf16[1024,8192]{1,0:T(8,128)(2,1)}, u32[]{:S(2)}) %copy-start.4) | copy-done | bytes 16777240
  61.2 4.2 %project.4 = (bf16[192,2048]{1,0:T(8,128)(2,1)S(1)}, bf16[192,2048]{1,0:T(8,128)(2,1)}) custom-call(s32[4]{0:T(128)S(1)} %pad_add_fusion.s, bf16[192,1024]{1,0:T(8,128)(2,1)S(1)} %copy-done.6, bf16[1024,8192]{1,0:T(8,128)(2,1)S(1)} %copy-done.4), custom_call_target="tpu_custom_call" | custom-call | tf_op jit(solution)/shard_map/project/pallas_call | solution.py:41
  65.3 1.1 collective-permute-done.5
  66.7 2.3 %collective-permute-start.6 = (bf16[192,1024]{1,0:T(8,128)(2,1)S(1)}, bf16[192,1024]{1,0:T(8,128)(2,1)S(1)}, u32[]{:S(2)}, u32[]{:S(2)}) collective-permute-start(bf16[192,1024]{1,0:T(8,128)(2,1)S(1)} %constant_dynamic-slice_fusion), channel_id=1, source_target_pairs={{0,1},{1,0},{2,3},{3,2},{4,5},{5,4},{6,7},{7,6},{8,9},{9,8},{10,11... | collective-permute-start | bytes 1179656 | tf_op jit(solution)/shard_map/ppermute | solution.py:197
  69.0 1.3 collective-permute-done.6
  70.6 0.4 collective-permute-start.7
  71.0 1.3 collective-permute-done.7
  72.6 1.9 collective-permute-start.8
  74.6 11.1 %collective-permute-done.8.refs_0_ = bf16[192,2048]{1,0:T(8,128)(2,1)S(1)} collective-permute-done((bf16[192,2048]{1,0:T(8,128)(2,1)S(1)}, bf16[192,2048]{1,0:T(8,128)(2,1)S(1)}, u32[]{:S(2)}, u32[]{:S(2)}) %collective-permute-start.8) | collective-permute-done | bytes 786464 | tf_op jit(solution)/shard_map/ppermute | solution.py:286
  85.7 1.9 collective-permute-start.9
  87.6 10.8 %collective-permute-done.9.refs_0_ = bf16[192,2048]{1,0:T(8,128)(2,1)S(1)} collective-permute-done((bf16[192,2048]{1,0:T(8,128)(2,1)S(1)}, bf16[192,2048]{1,0:T(8,128)(2,1)S(1)}, u32[]{:S(2)}, u32[]{:S(2)}) %collective-permute-start.9) | collective-permute-done | bytes 786464 | tf_op jit(solution)/shard_map/ppermute | solution.py:286
  98.4 2.0 collective-permute-start.10
  100.4 2.2 collective-permute-start.17
  102.5 1.3 collective-permute-start.20
  103.8 2.1 collective-permute-start.14
  106.0 3.2 %collective-permute-done.10.refs_0_ = bf16[192,2048]{1,0:T(8,128)(2,1)S(1)} collective-permute-done((bf16[192,2048]{1,0:T(8,128)(2,1)S(1)}, bf16[192,2048]{1,0:T(8,128)(2,1)S(1)}, u32[]{:S(2)}, u32[]{:S(2)}) %collective-permute-start.10) | collective-permute-done | bytes 786464 | tf_op jit(solution)/shard_map/ppermute | solution.py:286
  109.2 1.6 collective-permute-start.11
  110.8 19.4 %collective-permute-done.20 = bf16[192,1024]{1,0:T(8,128)(2,1)S(1)} collective-permute-done((bf16[192,1024]{1,0:T(8,128)(2,1)S(1)}, bf16[192,1024]{1,0:T(8,128)(2,1)S(1)}, u32[]{:S(2)}, u32[]{:S(2)}) %collective-permute-start.20) | collective-permute-done | bytes 393248 | tf_op jit(solution)/shard_map/ppermute | solution.py:275
  130.7 1.2 collective-permute-done.21
  132.4 6.1 %collective-permute-done.14.refs_1_ = bf16[192,2048]{1,0:T(8,128)(2,1)} collective-permute-done((bf16[192,2048]{1,0:T(8,128)(2,1)S(1)}, bf16[192,2048]{1,0:T(8,128)(2,1)}, u32[]{:S(2)}, u32[]{:S(2)}) %collective-permute-start.14) | collective-permute-done | bytes 786464 | tf_op jit(solution)/shard_map/ppermute | solution.py:275
  138.5 0.9 copy-done.7
  139.4 0.5 collective-permute-start.12
  140.1 6.5 %split_weight.4.refs_0_ = bf16[2,8192,1024]{2,1,0:T(8,128)(2,1)S(1)} custom-call(bf16[8192,2,1024]{2,1,0:T(2,128)(2,1)} %w_ref.15), custom_call_target="tpu_custom_call" | custom-call | tf_op jit(solution)/shard_map/split_weight/pallas_call | solution.py:77
  146.6 6.5 %split_weight.5.refs_0_ = bf16[2,8192,1024]{2,1,0:T(8,128)(2,1)S(1)} custom-call(bf16[8192,2,1024]{2,1,0:T(2,128)(2,1)} %w_ref.15, bf16[2,8192,1024]{2,1,0:T(8,128)(2,1)S(1)} %split_weight.4.refs_0_), custom_call_target="tpu_custom_call", output_to_operand_aliasing={{}: (1, {})} | custom-call | tf_op jit(solution)/shard_map/split_weight/pallas_call | solution.py:77
  153.1 6.5 %split_weight.6.refs_0_ = bf16[2,8192,1024]{2,1,0:T(8,128)(2,1)S(1)} custom-call(bf16[8192,2,1024]{2,1,0:T(2,128)(2,1)} %w_ref.15, bf16[2,8192,1024]{2,1,0:T(8,128)(2,1)S(1)} %split_weight.5.refs_0_), custom_call_target="tpu_custom_call", output_to_operand_aliasing={{}: (1, {})} | custom-call | tf_op jit(solution)/shard_map/split_weight/pallas_call | solution.py:77
  159.7 6.5 %split_weight.7.refs_3_.refs_5_ = bf16[2,8192,1024]{2,1,0:T(8,128)(2,1)S(1)} custom-call(bf16[8192,2,1024]{2,1,0:T(2,128)(2,1)} %w_ref.15, bf16[2,8192,1024]{2,1,0:T(8,128)(2,1)S(1)} %split_weight.6.refs_0_), custom_call_target="tpu_custom_call", output_to_operand_aliasing={{}: (1, {})} | custom-call | tf_op jit(solution)/shard_map/split_weight/pallas_call | solution.py:77
  166.2 11.1 %copy-done = bf16[2,8192,1024]{2,1,0:T(8,128)(2,1)} copy-done((bf16[2,8192,1024]{2,1,0:T(8,128)(2,1)}, bf16[2,8192,1024]{2,1,0:T(8,128)(2,1)S(1)}, u32[]{:S(2)}) %copy-start) | copy-done | bytes 33554456
  177.6 1.6 maximum_select_fusion.1.refs_1_
  179.2 7.2 %gate_products.4 = (f32[2,384,1024]{2,1,0:T(8,128)S(1)}, f32[384,1]{1,0:T(8,128)S(1)}) custom-call(s32[6]{0:T(128)S(1)} %stack.170.s, bf16[192,2048]{1,0:T(8,128)(2,1)S(1)} %maximum_select_fusion.refs_0_, bf16[192,2048]{1,0:T(8,128)(2,1)S(1)} %maximum_select_fusion.1.refs_1_, f32[1,8192]{1,0:T(1,128)S(1)} %bitcast.28, bf16[2,8192,1024]{2,1,0:T(8,128)(2,1)} %copy-done), custom_call_target="tpu_custom_call" | custom-call | tf_op jit(solution)/shard_map/gate_products/pallas_call | solution.py:184
  186.5 13.5 %gate_products.5 = (f32[2,384,1024]{2,1,0:T(8,128)S(1)}, f32[384,1]{1,0:T(8,128)S(1)}) custom-call(s32[6]{0:T(128)S(1)} %stack.169.s, bf16[192,2048]{1,0:T(8,128)(2,1)S(1)} %collective-permute-done.8.refs_0_, bf16[192,2048]{1,0:T(8,128)(2,1)} %collective-permute-done.17.refs_1_, ...), custom_call_target="tpu_custom_call", output_to_operand_aliasing={{0}: (7, {}), {1}: (8, {})} | custom-call | tf_op jit(solution)/shard_map/gate_products/pallas_call | solution.py:184
  200.0 10.0 %gate_products.6 = (f32[2,384,1024]{2,1,0:T(8,128)S(1)}, f32[384,1]{1,0:T(8,128)S(1)}) custom-call(s32[6]{0:T(128)S(1)} %stack.162.s, bf16[192,2048]{1,0:T(8,128)(2,1)S(1)} %collective-permute-done.9.refs_0_, bf16[192,2048]{1,0:T(8,128)(2,1)} %collective-permute-done.14.refs_1_, ...), custom_call_target="tpu_custom_call", output_to_operand_aliasing={{0}: (7, {}), {1}: (8, {})} | custom-call | tf_op jit(solution)/shard_map/gate_products/pallas_call | solution.py:184
  210.1 7.4 %gate_products.7 = bf16[384,1024]{1,0:T(8,128)(2,1)} custom-call(s32[6]{0:T(128)S(1)} %stack.155.s, bf16[192,2048]{1,0:T(8,128)(2,1)S(1)} %collective-permute-done.10.refs_0_, bf16[192,2048]{1,0:T(8,128)(2,1)} %collective-permute-done.11.refs_1_, bf16[192,2048]{1,0:T(8,128)(2,1)} %collective-permute-done.12.refs_2_, ...), custom_call_target="tpu_custom_call" | custom-call | tf_op jit(solution)/shard_map/gate_products/pallas_call | solution.py:184
  (53 shorter events, 2.9 us)
Async XLA Ops:
  0.8 5.8 %copy-start.1 = (bf16[1024,8192]{1,0:T(8,128)(2,1)S(1)}, bf16[1024,8192]{1,0:T(8,128)(2,1)}, u32[]{:S(2)}) copy-start(bf16[1024,8192]{1,0:T(8,128)(2,1)} %w_ref.11) | copy-start | bytes 50331652
  6.5 1.0 copy-start.5
  7.5 2.9 %copy-start.6 = (bf16[192,1024]{1,0:T(8,128)(2,1)S(1)}, bf16[192,1024]{1,0:T(8,128)(2,1)}, u32[]{:S(2)}) copy-start(bf16[192,1024]{1,0:T(8,128)(2,1)} %x_ref.7) | copy-start | bytes 1179652
  8.8 13.9 %collective-permute-start.2 = (bf16[192,2048]{1,0:T(8,128)(2,1)S(1)}, bf16[192,2048]{1,0:T(8,128)(2,1)}, u32[]{:S(2)}, u32[]{:S(2)}) collective-permute-start(bf16[192,2048]{1,0:T(8,128)(2,1)S(1)} %get-tuple-element.21), channel_id=1, source_target_pairs={{1,0},{12,13},{3,2},{14,15},{17,16},{28,29},{19,18},{30,31}} | collective-permute-start | bytes 2359304 | tf_op jit(solution)/shard_map/ppermute | solution.py:247
  10.5 5.8 %copy-start.2 = (bf16[1024,8192]{1,0:T(8,128)(2,1)S(1)}, bf16[1024,8192]{1,0:T(8,128)(2,1)}, u32[]{:S(2)}) copy-start(bf16[1024,8192]{1,0:T(8,128)(2,1)} %w_ref.11) | copy-start | bytes 50331652
  19.3 19.1 %collective-permute-start.1 = (bf16[192,2048]{1,0:T(8,128)(2,1)S(1)}, bf16[192,2048]{1,0:T(8,128)(2,1)}, u32[]{:S(2)}, u32[]{:S(2)}) collective-permute-start(bf16[192,2048]{1,0:T(8,128)(2,1)S(1)} %get-tuple-element.19), channel_id=1, source_target_pairs={{1,0},{5,4},{8,9},{12,13},{3,2},{7,6},{10,11},{14,15},{17,16},{21,... | collective-permute-start | bytes 2359304 | tf_op jit(solution)/shard_map/ppermute | solution.py:247
  25.0 13.4 %collective-permute-start.3 = (bf16[192,2048]{1,0:T(8,128)(2,1)}, bf16[192,2048]{1,0:T(8,128)(2,1)S(1)}, u32[]{:S(2)}, u32[]{:S(2)}) collective-permute-start(bf16[192,2048]{1,0:T(8,128)(2,1)} %add_convert_fusion.3), channel_id=1, source_target_pairs={{0,4},{13,9},{2,6},{15,11},{16,20},{29,25},{18,22},{31,27}} | collective-permute-start | bytes 2359304 | tf_op jit(solution)/shard_map/ppermute | solution.py:250
  25.9 5.8 %copy-start.3 = (bf16[1024,8192]{1,0:T(8,128)(2,1)S(1)}, bf16[1024,8192]{1,0:T(8,128)(2,1)}, u32[]{:S(2)}) copy-start(bf16[1024,8192]{1,0:T(8,128)(2,1)} %w_ref.11) | copy-start | bytes 50331652
  36.5 4.8 %collective-permute-start = (bf16[192,2048]{1,0:T(8,128)(2,1)S(1)}, bf16[192,2048]{1,0:T(8,128)(2,1)S(1)}, u32[]{:S(2)}, u32[]{:S(2)}) collective-permute-start(bf16[192,2048]{1,0:T(8,128)(2,1)S(1)} %get-tuple-element.17), channel_id=1, source_target_pairs={{1,0},{5,4},{9,8},{4,5},{8,9},{12,13},{3,2},{7,6},{11,10},{6,7},{1... | collective-permute-start | bytes 2359304 | tf_op jit(solution)/shard_map/ppermute | solution.py:247
  40.0 13.0 %collective-permute-start.4 = (bf16[192,2048]{1,0:T(8,128)(2,1)S(1)}, bf16[192,2048]{1,0:T(8,128)(2,1)S(1)}, u32[]{:S(2)}, u32[]{:S(2)}) collective-permute-start(bf16[192,2048]{1,0:T(8,128)(2,1)S(1)} %add_convert_fusion.2), channel_id=1, source_target_pairs={{0,4},{4,8},{9,5},{13,9},{2,6},{6,10},{11,7},{15,11},{16,20},{20,2... | collective-permute-start | bytes 2359304 | tf_op jit(solution)/shard_map/ppermute | solution.py:250
  53.4 13.0 %collective-permute-start.5 = (bf16[192,2048]{1,0:T(8,128)(2,1)S(1)}, bf16[192,2048]{1,0:T(8,128)(2,1)S(1)}, u32[]{:S(2)}, u32[]{:S(2)}) collective-permute-start(bf16[192,2048]{1,0:T(8,128)(2,1)S(1)} %add_convert_fusion.1), channel_id=1, source_target_pairs={{0,4},{4,8},{8,12},{5,1},{9,5},{13,9},{2,6},{6,10},{10,14},{7,3},{... | collective-permute-start | bytes 2359304 | tf_op jit(solution)/shard_map/ppermute | solution.py:250
  55.4 5.8 %copy-start.4 = (bf16[1024,8192]{1,0:T(8,128)(2,1)S(1)}, bf16[1024,8192]{1,0:T(8,128)(2,1)}, u32[]{:S(2)}) copy-start(bf16[1024,8192]{1,0:T(8,128)(2,1)} %w_ref.11) | copy-start | bytes 50331652
  66.4 3.9 %copy-start.10 = (bf16[192,1024]{1,0:T(8,128)(2,1)S(1)}, bf16[192,1024]{1,0:T(8,128)(2,1)}, u32[]{:S(2)}) copy-start(bf16[192,1024]{1,0:T(8,128)(2,1)} %param.6) | copy-start | bytes 1179652
  66.7 3.6 %collective-permute-start.6 = (bf16[192,1024]{1,0:T(8,128)(2,1)S(1)}, bf16[192,1024]{1,0:T(8,128)(2,1)S(1)}, u32[]{:S(2)}, u32[]{:S(2)}) collective-permute-start(bf16[192,1024]{1,0:T(8,128)(2,1)S(1)} %constant_dynamic-slice_fusion), channel_id=1, source_target_pairs={{0,1},{1,0},{2,3},{3,2},{4,5},{5,4},{6,7},{7,6},{8,9},{9,8},{10,11... | collective-permute-start | bytes 1179656 | tf_op jit(solution)/shard_map/ppermute | solution.py:197
  70.6 69.3 %copy-start.9 = (bf16[192,1024]{1,0:T(8,128)(2,1)}, bf16[192,1024]{1,0:T(8,128)(2,1)S(1)}, u32[]{:S(2)}) copy-start(bf16[192,1024]{1,0:T(8,128)(2,1)S(1)} %add_convert_fusion.4) | copy-start | bytes 1179652
  70.6 1.8 collective-permute-start.7
  72.6 13.0 %collective-permute-start.8 = (bf16[192,2048]{1,0:T(8,128)(2,1)S(1)}, bf16[192,2048]{1,0:T(8,128)(2,1)S(1)}, u32[]{:S(2)}, u32[]{:S(2)}) collective-permute-start(bf16[192,2048]{1,0:T(8,128)(2,1)S(1)} %maximum_select_fusion.refs_0_), channel_id=1, source_target_pairs={{0,4},{4,8},{8,12},{5,1},{9,5},{13,9},{2,6},{6,10},{10,14},{7,3},{... | collective-permute-start | bytes 2359304 | tf_op jit(solution)/shard_map/ppermute | solution.py:286
  85.7 12.7 %collective-permute-start.9 = (bf16[192,2048]{1,0:T(8,128)(2,1)S(1)}, bf16[192,2048]{1,0:T(8,128)(2,1)S(1)}, u32[]{:S(2)}, u32[]{:S(2)}) collective-permute-start(bf16[192,2048]{1,0:T(8,128)(2,1)S(1)} %collective-permute-done.8.refs_0_), channel_id=1, source_target_pairs={{4,8},{8,12},{5,1},{9,5},{6,10},{10,14},{7,3},{11,7},{20,24},{24,2... | collective-permute-start | bytes 2359304 | tf_op jit(solution)/shard_map/ppermute | solution.py:286
  98.4 10.8 %collective-permute-start.10 = (bf16[192,2048]{1,0:T(8,128)(2,1)S(1)}, bf16[192,2048]{1,0:T(8,128)(2,1)S(1)}, u32[]{:S(2)}, u32[]{:S(2)}) collective-permute-start(bf16[192,2048]{1,0:T(8,128)(2,1)S(1)} %collective-permute-done.9.refs_0_), channel_id=1, source_target_pairs={{8,12},{5,1},{10,14},{7,3},{24,28},{21,17},{26,30},{23,19}} | collective-permute-start | bytes 2359304 | tf_op jit(solution)/shard_map/ppermute | solution.py:286
  100.4 30.3 %collective-permute-start.17 = (bf16[192,2048]{1,0:T(8,128)(2,1)S(1)}, bf16[192,2048]{1,0:T(8,128)(2,1)}, u32[]{:S(2)}, u32[]{:S(2)}) collective-permute-start(bf16[192,2048]{1,0:T(8,128)(2,1)S(1)} %collective-permute-done.8.refs_0_), channel_id=1, source_target_pairs={{4,6},{6,4},{8,10},{10,8},{12,14},{14,12},{1,3},{3,1},{5,7},{7,5},... | collective-permute-start | bytes 2359304 | tf_op jit(solution)/shard_map/ppermute | solution.py:275
  102.5 27.7 %collective-permute-start.20 = (bf16[192,1024]{1,0:T(8,128)(2,1)S(1)}, bf16[192,1024]{1,0:T(8,128)(2,1)S(1)}, u32[]{:S(2)}, u32[]{:S(2)}) collective-permute-start(bf16[192,1024]{1,0:T(8,128)(2,1)S(1)} %add_convert_fusion.4), channel_id=1, source_target_pairs={{0,2},{2,0},{1,3},{3,1},{4,6},{6,4},{5,7},{7,5},{8,10},{10,8},{9,1... | collective-permute-start | bytes 1179656 | tf_op jit(solution)/shard_map/ppermute | solution.py:275
  103.8 34.7 %collective-permute-start.14 = (bf16[192,2048]{1,0:T(8,128)(2,1)S(1)}, bf16[192,2048]{1,0:T(8,128)(2,1)}, u32[]{:S(2)}, u32[]{:S(2)}) collective-permute-start(bf16[192,2048]{1,0:T(8,128)(2,1)S(1)} %collective-permute-done.9.refs_0_), channel_id=1, source_target_pairs={{8,10},{10,8},{12,14},{14,12},{1,3},{3,1},{5,7},{7,5},{24,26},{26,... | collective-permute-start | bytes 2359304 | tf_op jit(solution)/shard_map/ppermute | solution.py:275
  106.0 32.5 %collective-permute-start.18 = (bf16[192,2048]{1,0:T(8,128)(2,1)S(1)}, bf16[192,2048]{1,0:T(8,128)(2,1)S(1)}, u32[]{:S(2)}, u32[]{:S(2)}) collective-permute-start(bf16[192,2048]{1,0:T(8,128)(2,1)S(1)} %collective-permute-done.8.refs_0_), channel_id=1, source_target_pairs={{0,1},{1,0},{2,3},{3,2},{4,5},{5,4},{6,7},{7,6},{8,9},{9,8},{10,11... | collective-permute-start | bytes 2359304 | tf_op jit(solution)/shard_map/ppermute | solution.py:197
  109.2 30.6 %collective-permute-start.11 = (bf16[192,2048]{1,0:T(8,128)(2,1)S(1)}, bf16[192,2048]{1,0:T(8,128)(2,1)}, u32[]{:S(2)}, u32[]{:S(2)}) collective-permute-start(bf16[192,2048]{1,0:T(8,128)(2,1)S(1)} %collective-permute-done.10.refs_0_), channel_id=1, source_target_pairs={{12,14},{14,12},{1,3},{3,1},{28,30},{30,28},{17,19},{19,17}} | collective-permute-start | bytes 2359304 | tf_op jit(solution)/shard_map/ppermute | solution.py:275
  130.2 9.7 %copy-start.11 = (bf16[192,1024]{1,0:T(8,128)(2,1)}, bf16[192,1024]{1,0:T(8,128)(2,1)S(1)}, u32[]{:S(2)}) copy-start(bf16[192,1024]{1,0:T(8,128)(2,1)S(1)} %collective-permute-done.20) | copy-start | bytes 1179652
  130.2 1.8 collective-permute-start.21
  130.6 55.8 %collective-permute-start.19 = (bf16[192,2048]{1,0:T(8,128)(2,1)}, bf16[192,2048]{1,0:T(8,128)(2,1)}, u32[]{:S(2)}, u32[]{:S(2)}) collective-permute-start(bf16[192,2048]{1,0:T(8,128)(2,1)} %collective-permute-done.17.refs_1_), channel_id=1, source_target_pairs={{0,1},{1,0},{2,3},{3,2},{4,5},{5,4},{6,7},{7,6},{8,9},{9,8},{10,11... | collective-permute-start | bytes 2359304 | tf_op jit(solution)/shard_map/ppermute | solution.py:197
  132.0 7.9 %copy-start.12 = (bf16[192,1024]{1,0:T(8,128)(2,1)}, bf16[192,1024]{1,0:T(8,128)(2,1)S(1)}, u32[]{:S(2)}) copy-start(bf16[192,1024]{1,0:T(8,128)(2,1)S(1)} %collective-permute-done.21) | copy-start | bytes 1179652
  132.0 68.0 %collective-permute-start.15 = (bf16[192,2048]{1,0:T(8,128)(2,1)S(1)}, bf16[192,2048]{1,0:T(8,128)(2,1)}, u32[]{:S(2)}, u32[]{:S(2)}) collective-permute-start(bf16[192,2048]{1,0:T(8,128)(2,1)S(1)} %collective-permute-done.9.refs_0_), channel_id=1, source_target_pairs={{0,1},{1,0},{2,3},{3,2},{4,5},{5,4},{6,7},{7,6},{8,9},{9,8},{10,11... | collective-permute-start | bytes 2359304 | tf_op jit(solution)/shard_map/ppermute | solution.py:197
  138.5 61.5 %collective-permute-start.16 = (bf16[192,2048]{1,0:T(8,128)(2,1)}, bf16[192,2048]{1,0:T(8,128)(2,1)}, u32[]{:S(2)}, u32[]{:S(2)}) collective-permute-start(bf16[192,2048]{1,0:T(8,128)(2,1)} %collective-permute-done.14.refs_1_), channel_id=1, source_target_pairs={{0,1},{1,0},{2,3},{3,2},{4,5},{5,4},{6,7},{7,6},{8,9},{9,8},{10,11... | collective-permute-start | bytes 2359304 | tf_op jit(solution)/shard_map/ppermute | solution.py:197
  138.5 0.9 copy-start.7
  139.4 70.7 %collective-permute-start.12 = (bf16[192,2048]{1,0:T(8,128)(2,1)S(1)}, bf16[192,2048]{1,0:T(8,128)(2,1)}, u32[]{:S(2)}, u32[]{:S(2)}) collective-permute-start(bf16[192,2048]{1,0:T(8,128)(2,1)S(1)} %collective-permute-done.10.refs_0_), channel_id=1, source_target_pairs={{0,1},{1,0},{2,3},{3,2},{4,5},{5,4},{6,7},{7,6},{8,9},{9,8},{10,11... | collective-permute-start | bytes 2359304 | tf_op jit(solution)/shard_map/ppermute | solution.py:197
  139.9 70.2 %collective-permute-start.13 = (bf16[192,2048]{1,0:T(8,128)(2,1)}, bf16[192,2048]{1,0:T(8,128)(2,1)}, u32[]{:S(2)}, u32[]{:S(2)}) collective-permute-start(bf16[192,2048]{1,0:T(8,128)(2,1)} %collective-permute-done.11.refs_1_), channel_id=1, source_target_pairs={{0,1},{1,0},{2,3},{3,2},{4,5},{5,4},{6,7},{7,6},{8,9},{9,8},{10,11... | collective-permute-start | bytes 2359304 | tf_op jit(solution)/shard_map/ppermute | solution.py:197
  159.7 17.6 %copy-start.13 = (bf16[8192]{0:T(1024)(128)(2,1)S(1)}, bf16[8192]{0:T(1024)(128)(2,1)}, u32[]{:S(2)}) copy-start(bf16[8192]{0:T(1024)(128)(2,1)} %param.8) | copy-start | bytes 49156
  166.2 11.1 %copy-start = (bf16[2,8192,1024]{2,1,0:T(8,128)(2,1)}, bf16[2,8192,1024]{2,1,0:T(8,128)(2,1)S(1)}, u32[]{:S(2)}) copy-start(bf16[2,8192,1024]{2,1,0:T(8,128)(2,1)S(1)} %split_weight.7.refs_3_.refs_5_) | copy-start | bytes 100663296
  179.2 7.3 %copy-start.8 = (bf16[192,2048]{1,0:T(8,128)(2,1)S(1)}, bf16[192,2048]{1,0:T(8,128)(2,1)}, u32[]{:S(2)}) copy-start(bf16[192,2048]{1,0:T(8,128)(2,1)} %copy-done.7) | copy-start | bytes 2359300

commit v2 on v1

v2 whole, which is shorter than its diff:
```python
import math

import jax
import jax.numpy as jnp
import numpy as np
from jax import lax
from jax.experimental import pallas as pl
from jax.experimental.pallas import tpu as pltpu
from jax.sharding import PartitionSpec as P


EPSILON = 1e-06
BF16 = jnp.bfloat16
F32 = jnp.float32
LINE = ("tensor", "section")
RELAYOUT_CALLS = 4
LONGEST_LINE = 8
SMALL = 6 << 20
LARGE = 17 << 20


def tile_of(size, limit):
    return math.gcd(size, limit)


def hbm(x):
    return pltpu.with_memory_space_constraint(x, pltpu.HBM)


def vmem(x):
    return pltpu.with_memory_space_constraint(x, pltpu.VMEM)


def project(table, at, count, attn_out, out_weight, width):
    rows, depth = attn_out.shape
    tile = tile_of(width, 1024)
    tiles = width // tile

    def body(s, x_ref, w_ref, out_ref):
        out_ref[...] = jnp.dot(x_ref[...], w_ref[...], preferred_element_type=F32).astype(BF16)

    return pl.pallas_call(
        body,
        grid_spec=pltpu.PrefetchScalarGridSpec(
            num_scalar_prefetch=1,
            grid=(count, tiles),
            in_specs=[
                pl.BlockSpec((rows, depth), lambda j, t, s: (0, 0)),
                pl.BlockSpec((depth, tile), lambda j, t, s: (0, s[at + j] * tiles + t)),
            ],
            out_specs=pl.BlockSpec((None, rows, tile), lambda j, t, s: (j, 0, t)),
        ),
        out_shape=jax.ShapeDtypeStruct((count, rows, width), BF16),
        compiler_params=pltpu.CompilerParams(vmem_limit_bytes=12 << 20),
        name="project",
    )(table, attn_out, hbm(out_weight))


def add_up(terms):
    arrays = [term[0] if isinstance(term, tuple) else term for term in terms]
    rows, width = arrays[0].shape[-2:]
    tile = tile_of(width, 1024)
    specs = []
    for term in terms:
        if isinstance(term, tuple):
            specs.append(pl.BlockSpec((None, rows, tile), lambda t, k=term[1]: (k, 0, t)))
        else:
            specs.append(pl.BlockSpec((rows, tile), lambda t: (0, t)))

    def body(*refs):
        refs[-1][...] = sum(ref[...].astype(F32) for ref in refs[:-1]).astype(BF16)

    return pl.pallas_call(
        body,
        grid=(width // tile,),
        in_specs=specs,
        out_specs=pl.BlockSpec((rows, tile), lambda t: (0, t)),
        out_shape=jax.ShapeDtypeStruct((rows, width), BF16),
        compiler_params=pltpu.CompilerParams(vmem_limit_bytes=SMALL),
        name="add_up",
    )(*arrays)


def prepare(table, at, count, base, mine, theirs):
    rows, width = base.shape
    tile = tile_of(width, 1024)

    def plane(r, t, s):
        return jnp.maximum(s[at + r] - 1, 0), 0, t

    def body(s, base_ref, mine_ref, theirs_ref, out_ref):
        both = mine_ref[...].astype(F32) + theirs_ref[...].astype(F32)
        out_ref[...] = jnp.where(s[at + pl.program_id(0)] == 0, base_ref[...].astype(F32), both).astype(BF16)

    return pl.pallas_call(
        body,
        grid_spec=pltpu.PrefetchScalarGridSpec(
            num_scalar_prefetch=1,
            grid=(count, width // tile),
            in_specs=[pl.BlockSpec((rows, tile), lambda r, t, s: (0, t))] + [pl.BlockSpec((None, rows, tile), plane)] * 2,
            out_specs=pl.BlockSpec((None, rows, tile), lambda r, t, s: (r, 0, t)),
        ),
        out_shape=jax.ShapeDtypeStruct((count, rows, width), BF16),
        compiler_params=pltpu.CompilerParams(vmem_limit_bytes=SMALL),
        name="prepare",
    )(table, base, mine, theirs)


def pair(table, core_at, mine, theirs):
    rows, shard = mine.shape

    def body(s, mine_ref, theirs_ref, out_ref):
        core = s[core_at]

        @pl.when(core == 0)
        def _():
            out_ref[:, :shard] = mine_ref[...]
            out_ref[:, shard:] = theirs_ref[...]

        @pl.when(core != 0)
        def _():
            out_ref[:, :shard] = theirs_ref[...]
            out_ref[:, shard:] = mine_ref[...]

    spec = pl.BlockSpec((rows, shard), lambda i, s: (0, 0))
    return pl.pallas_call(
        body,
        grid_spec=pltpu.PrefetchScalarGridSpec(
            num_scalar_prefetch=1,
            grid=(1,),
            in_specs=[spec, spec],
            out_specs=pl.BlockSpec((rows, 2 * shard), lambda i, s: (0, 0)),
        ),
        out_shape=jax.ShapeDtypeStruct((rows, 2 * shard), BF16),
        compiler_params=pltpu.CompilerParams(vmem_limit_bytes=SMALL),
        name="pair",
    )(table, mine, theirs)


def finish_stream(table, core_at, mine, theirs, residual):
    rows, width = mine.shape
    shard = width // 2

    def body(s, mine_ref, theirs_ref, residual_ref, block_ref, half_ref):
        sums = mine_ref[...].astype(F32) + theirs_ref[...].astype(F32)
        block = (sums + residual_ref[...].astype(F32)).astype(BF16)
        block_ref[...] = block
        half_ref[...] = jnp.where(s[core_at] == 0, block[:, :shard], block[:, shard:])

    spec = pl.BlockSpec((rows, width), lambda i, s: (0, 0))
    return pl.pallas_call(
        body,
        grid_spec=pltpu.PrefetchScalarGridSpec(
            num_scalar_prefetch=1,
            grid=(1,),
            in_specs=[spec] * 3,
            out_specs=[spec, pl.BlockSpec((rows, shard), lambda i, s: (0, 0))],
        ),
        out_shape=[jax.ShapeDtypeStruct((rows, width), BF16), jax.ShapeDtypeStruct((rows, shard), BF16)],
        compiler_params=pltpu.CompilerParams(vmem_limit_bytes=SMALL),
        name="finish_stream",
    )(table, mine, theirs, residual)


def split_weight(gate_up, buffer, call, calls):
    depth, _, cols = gate_up.shape
    span = depth // calls
    tile = tile_of(span, 1024)
    steps = span // tile

    def body(w_ref, *refs):
        refs[-1][...] = jnp.swapaxes(w_ref[...], 0, 1)

    operands = [hbm(gate_up)]
    in_specs = [pl.BlockSpec((tile, 2, cols), lambda i: (call * steps + i, 0, 0))]
    aliases = {}
    if buffer is not None:
        operands.append(vmem(buffer))
        in_specs.append(pl.BlockSpec(memory_space=pl.ANY))
        aliases = {1: 0}
    return pl.pallas_call(
        body,
        grid=(steps,),
        in_specs=in_specs,
        out_specs=pl.BlockSpec((2, tile, cols), lambda i: (0, call * steps + i, 0)),
        out_shape=jax.ShapeDtypeStruct((2, depth, cols), BF16),
        input_output_aliases=aliases,
        compiler_params=pltpu.CompilerParams(vmem_limit_bytes=LARGE),
        name="split_weight",
    )(*operands)


def gate_products(table, at, places_at, blocks, gain, weight, carry, final):
    chunks = len(blocks[0])
    rows, width = blocks[0][0].shape
    _, depth, cols = weight.shape
    tile = tile_of(width, 1024)
    tiles = width // tile
    total = chunks * rows
    sides = len(blocks)

    def block_at(j, t, s):
        index = s[at] * tiles + t
        for side in range(sides - 1, -1, -1):
            others = [k for k in range(sides) if k != side]
            here = s[at + side] * tiles + t
            if others:
                other = others[0]
                stay = s[at + other] * tiles + (0 if side == 0 else tiles - 1)
                here = jnp.where(s[at + 2 + side] > 0, here, jnp.where(s[at + 2 + other] > 0, stay, 0))
            index = here if side == sides - 1 else jnp.where(j == side, here, index)
        return index

    def chunk_spec(side):
        def chunk_at(j, t, s):
            return 0, jnp.where(j == side, t, 0 if side else tiles - 1)

        return pl.BlockSpec((rows, tile), chunk_at)

    first = carry is None

    def body(s, *refs):
        refs = list(refs)
        x_refs = [[refs.pop(0) for _ in range(chunks)] for _ in range(sides)]
        gain_ref, w_ref = refs.pop(0), refs.pop(0)
        if not first:
            acc_in, sq_in = refs.pop(0), refs.pop(0)
        if final:
            out_ref, staged, acc, squares = refs
        else:
            acc, squares, _, staged = refs
        j, t = pl.program_id(0), pl.program_id(1)

        @pl.when((j == 0) & (t == 0))
        def _():
            if first:
                acc[...] = jnp.zeros_like(acc)
                squares[...] = jnp.zeros_like(squares)
            else:
                acc[...] = acc_in[...]
                squares[...] = sq_in[...]

        for side in range(sides):

            @pl.when((j == side) & (s[at + 2 + side] > 0))
            def _():
                for chunk in range(chunks):
                    x = x_refs[side][chunk][...].astype(F32)
                    span = pl.ds(chunk * rows, rows)
                    squares[span, :] += jnp.sum(x * x, axis=1, keepdims=True)
                    staged[span, :] = (x * gain_ref[...].astype(F32)).astype(BF16)
                at_row = pl.multiple_of((s[at + side] * tiles + t) * tile, tile)
                for half in range(2):
                    acc[half] += jnp.dot(staged[...], w_ref[half, pl.ds(at_row, tile), :], preferred_element_type=F32)

        if final:

            @pl.when((j == sides - 1) & (t == tiles - 1))
            def _():
                for chunk in range(chunks):
                    span = pl.ds(chunk * rows, rows)
                    scale = lax.rsqrt(squares[span, :] / depth + EPSILON)
                    gate = acc[0, span, :] * scale
                    up = acc[1, span, :] * scale
                    out_ref[pl.ds(s[places_at + chunk] * rows, rows), :] = (gate / (1.0 + jnp.exp(-gate)) * up).astype(BF16)

    acc_shape, sq_shape = (2, total, cols), (total, 1)
    operands = [*blocks[0]] + ([*blocks[1]] if sides > 1 else []) + [gain, vmem(weight)]
    in_specs = [chunk_spec(side) for side in range(sides) for _ in range(chunks)] + [
        pl.BlockSpec((1, tile), lambda j, t, s: (0, block_at(j, t, s))),
        pl.BlockSpec(memory_space=pltpu.VMEM),
    ]
    acc_spec = pl.BlockSpec(acc_shape, lambda j, t, s: (0, 0, 0))
    sq_spec = pl.BlockSpec(sq_shape, lambda j, t, s: (0, 0))
    aliases = {} if final else {len(operands): 2}
    if not first:
        if not final:
            aliases |= {1 + len(operands): 0, 2 + len(operands): 1}
        operands += list(carry)
        in_specs += [acc_spec, sq_spec]
    scratch = [pltpu.VMEM((total, tile), BF16)]
    if final:
        out_shape = jax.ShapeDtypeStruct((total, cols), BF16)
        out_specs = pl.BlockSpec((total, cols), lambda j, t, s: (0, 0))
        scratch += [pltpu.VMEM(acc_shape, F32), pltpu.VMEM(sq_shape, F32)]
    else:
        out_shape = [jax.ShapeDtypeStruct(shape, F32) for shape in (acc_shape, sq_shape)]
        out_shape.append(jax.ShapeDtypeStruct(weight.shape, BF16))
        out_specs = [acc_spec, sq_spec, pl.BlockSpec(memory_space=pl.ANY)]
    return pl.pallas_call(
        body,
        grid_spec=pltpu.PrefetchScalarGridSpec(
            num_scalar_prefetch=1, grid=(sides, tiles), in_specs=in_specs, out_specs=out_specs, scratch_shapes=scratch
        ),
        out_shape=out_shape,
        input_output_aliases=aliases,
        compiler_params=pltpu.CompilerParams(vmem_limit_bytes=LARGE - 4096),
        name="gate_products",
    )(table, *operands)


def swap_cores(x):
    return lax.ppermute(x, "section", [(0, 1), (1, 0)])


def layout_of(line, cores, replicas):
    order = [sorted((b for b in range(line) if b != k), key=lambda b: (-abs(b - k), -b)) + [k] for k in range(line)]
    rows = []
    for z in range(line):
        for core in range(cores):
            for x in range(replicas):
                row = list(order[z])
                for r in range(2, line):
                    up = order[z].index(z + line - r) if z < r else None
                    down = order[z].index(z - line + r) if z >= line - r else None
                    wanted = (up, down) if core == 0 else (down, up)
                    row.append(next((slot for slot in wanted if slot is not None), 0))
                row.append(core)
                row += [z, 0, 1, 0]
                for r in range(1, line):
                    pair_of = (z - r, z + r) if core == 0 else (z + r, z - r)
                    row += [b % line for b in pair_of] + [int(0 <= b < line) for b in pair_of]
                row += [(x - shift) % replicas for shift in range(replicas)]
                rows.append(row)
    starts = dict(order=0, slots=line, core=2 * line - 2, gates=2 * line - 1, places=6 * line - 1)
    return np.asarray(rows, np.int32), starts


def long_line(attn_out, residual, out_weight, norm_gain, gate_up):
    size, position = lax.axis_size(LINE), lax.axis_index(LINE)
    row_count, shard = attn_out.shape
    blocked = jnp.dot(attn_out, out_weight, preferred_element_type=F32).astype(BF16).reshape(row_count, size, shard)
    for level in range(size.bit_length() - 1):
        paired = blocked.reshape(row_count, blocked.shape[1] // 2, 2, shard)
        bit = position >> level & 1
        kept = lax.dynamic_index_in_dim(paired, bit, 2, keepdims=False)
        sent = lax.dynamic_index_in_dim(paired, 1 - bit, 2, keepdims=False)
        received = lax.ppermute(sent, LINE, [(i, i ^ 1 << level) for i in range(size)])
        blocked = (kept.astype(F32) + received.astype(F32)).astype(BF16)
    stream = (blocked.reshape(row_count, shard).astype(F32) + residual.astype(F32)).astype(BF16)
    wide = lax.all_gather(stream, LINE, axis=1, tiled=True).astype(F32)
    depth, _, cols = gate_up.shape
    mean_square = jnp.sum(wide * wide, axis=1, keepdims=True) / depth
    normed = (wide * lax.rsqrt(mean_square + EPSILON) * norm_gain.astype(F32)).astype(BF16)
    normed = lax.all_gather(normed, "seq", axis=0, tiled=True)
    products = jnp.dot(normed, gate_up.reshape(depth, 2 * cols), preferred_element_type=F32)
    products = products.reshape(normed.shape[0], 2, cols)
    return stream, (jax.nn.silu(products[:, 0]) * products[:, 1]).astype(BF16)


def local(attn_out, residual, out_weight, norm_gain, gate_up):
    if lax.axis_size("tensor") > LONGEST_LINE:
        return long_line(attn_out, residual, out_weight, norm_gain, gate_up)
    line, cores, replicas = (lax.axis_size(name) for name in ("tensor", "section", "seq"))
    z, core, x = (lax.axis_index(name) for name in ("tensor", "section", "seq"))
    _, shard = attn_out.shape
    width = shard * cores
    rows_of, starts = layout_of(line, cores, replicas)
    table = lax.dynamic_index_in_dim(jnp.asarray(rows_of), (z * cores + core) * replicas + x, 0, keepdims=False)
    core_at = starts["core"]

    first = project(table, 0, 1, attn_out, out_weight, width)
    first_pair = swap_cores(first)
    base = add_up([(first, 0), (first_pair, 0)])
    rest = project(table, 1, line - 1, attn_out, out_weight, width)
    rest_pair = swap_cores(rest)
    bases = prepare(table, starts["slots"], line - 2, base, rest, rest_pair)
    residual_pair = swap_cores(residual)
    residual = pair(table, core_at, residual, residual_pair)
    moving = base
    for r in range(1, line):
        pairs = [(2 * k, 2 * k + 2) for k in range(r)] + [(2 * k + 1, 2 * k - 1) for k in range(line - r, line)]
        received = lax.ppermute(moving, LINE, pairs)
        moving = add_up([(bases, r - 1) if r < line - 1 else (rest, line - 2), received])
    block, stream = finish_stream(table, core_at, moving, swap_cores(moving), residual)

    weight = None
    for call in range(RELAYOUT_CALLS):
        weight = split_weight(gate_up, weight, call, RELAYOUT_CALLS)
    gain = norm_gain.reshape(1, -1)

    def across(a, senders):
        out = []
        for shift in range(1, replicas):
            pairs = []
            for device in senders:
                for k in range(replicas):
                    there = (k + shift) % replicas
                    k_at, c_at = divmod(device, cores)
                    pairs.append(((k_at * replicas + k) * cores + c_at, (k_at * replicas + there) * cores + c_at))
            out.append(lax.ppermute(a, ("tensor", "seq", "section"), pairs))
        return out

    crossed = across(stream, range(line * cores))
    crossed = [pair(table, core_at, a, swap_cores(a)) for a in crossed]

    def gate(r, blocks, weight, carry):
        at = starts["gates"] + 4 * r
        return gate_products(table, at, starts["places"], blocks, gain, weight, carry, r == line - 1)

    *carry, weight = gate(0, [[block, *crossed]], weight, None)
    moving = block
    for r in range(1, line):
        pairs = [(2 * k, 2 * k + 2) for k in range(r - 1, line - 1)]
        pairs += [(2 * k + 1, 2 * k - 1) for k in range(1, line - r + 1)]
        moving = lax.ppermute(moving, LINE, pairs)
        holders = [2 * k for k in range(r, line)] + [2 * k + 1 for k in range(0, line - r)]
        crossed = across(moving, holders)
        other = swap_cores(moving)
        others = [swap_cores(a) for a in crossed]
        result = gate(r, [[moving, *crossed], [other, *others]], weight, carry)
        if r < line - 1:
            *carry, weight = result
    return stream, result


def solution(mesh):
    placed = (
        P(("groups", "seq"), ("tensor", "section")),
        P(("groups", "seq"), ("tensor", "section")),
        P(("tensor", "section"), None),
        P(),
        P(None, None, ("tensor", "seq", "section")),
    )
    return jax.shard_map(
        local,
        mesh=mesh,
        in_specs=placed,
        out_specs=(
            P(("groups", "seq"), ("tensor", "section")),
            P("groups", ("tensor", "seq", "section")),
        ),
        check_vma=False,
    )
```

time: 219 us -> 225 us (1.027)
  waiting for transfers between devices: 67.4 us -> 89.6 us
  Pallas kernels: 77.5 us -> 65.6 us
  local copies, waits for them, and re-layouts: 36.4 us -> 46.6 us
  other arithmetic: 6.88 us -> 0 us
  starting transfers between devices: 28.1 us -> 21.4 us
    ppermute x6 -> x3, waiting for transfers between devices: 12.8 us -> 32.8 us  [local(): received = lax.ppermute(moving, LINE, pairs)]
    unnamed x28 -> x16, local copies, waits for them, and re-layouts: 36 us -> 45.8 us
    pallas_call x4, Pallas kernels: 38.2 us -> 29.5 us  [gate_products(): pl.pallas_call(body, grid_spec=pltpu.PrefetchScalarGridSpec(num_scalar_pr...]
    pallas_call x4, Pallas kernels: 26 us -> 18.1 us  [split_weight(): pl.pallas_call(body, grid=(steps,), in_specs=in_specs, out_specs=pl.Block...]
    ppermute x6 -> x3, starting transfers between devices: 10.9 us -> 3.92 us  [local(): received = lax.ppermute(moving, LINE, pairs)]
    pallas_call x0 -> x8, Pallas kernels: none -> 6.33 us  [the longest x1 1.78 us: prepare(): pl.pallas_call(body, grid_spec=pltpu.PrefetchScalarGridSpec(num_scalar_pr...]
    convert_element_type x5 -> x0, other arithmetic: 4.66 us -> none  [add(): return sum((term.astype(F32) for term in terms)).astype(BF16)]
    ppermute x9 -> x11, waiting for transfers between devices: 3.96 us -> 5.88 us  [swap_cores(): return lax.ppermute(x, 'section', [(0, 1), (1, 0)])]
  transfers between devices with their start and end apart: 22 -> 21, of which waited for: 10 -> 10; matrix products, arithmetic and copies ran while one was open for 3% -> 0% of each run, Pallas kernels for 32% -> 22%
where the time goes in v2:
time: 225 us; the launch traced here: 224 us
  waiting for transfers between devices  89.6 us (40%)
  Pallas kernels  65.6 us (29%)
  local copies, waits for them, and re-layouts  46.6 us (21%)
  starting transfers between devices  21.4 us (10%)
    unnamed x16, local copies, waits for them, and re-layouts  45.8 us
    ppermute x3, waiting for transfers between devices, local(): received = lax.ppermute(moving, LINE, pairs)  32.8 us
    pallas_call x4, Pallas kernels, gate_products(): pl.pallas_call(body, grid_spec=pltpu.PrefetchScalarGridSpec(num_scalar_pr...  29.5 us
    ppermute x4, waiting for transfers between devices, across(): out.append(lax.ppermute(a, ('tensor', 'seq', 'section'), pairs))  25.7 us
    ppermute x3, waiting for transfers between devices, local(): moving = lax.ppermute(moving, LINE, pairs)  25.1 us
    pallas_call x4, Pallas kernels, split_weight(): pl.pallas_call(body, grid=(steps,), in_specs=in_specs, out_specs=pl.Block...  18.1 us
    pallas_call x2, Pallas kernels, project(): pl.pallas_call(body, grid_spec=pltpu.PrefetchScalarGridSpec(num_scalar_pr...  11.6 us
    ppermute x4, starting transfers between devices, across(): out.append(lax.ppermute(a, ('tensor', 'seq', 'section'), pairs))  6.25 us
  transfers between devices with their start and end apart: 21, of which 10 were waited for; matrix products, arithmetic and copies ran while one was open for 0% of the time, Pallas kernels for 22%

profile of v2, /device:TPU:15, one launch (start us, length us, event | category | flops | bytes accessed | tf_op | source)
XLA Modules:
  0.0 224.0 jit_solution(16160415422026524526)
XLA Ops:
  0.6 0.7 dynamic-slice_bitcast_fusion.s
  1.3 1.0 copy-done.5
  2.3 8.2 %project.2.mine_ref.refs_0_ = bf16[3,192,2048]{2,1,0:T(8,128)(2,1)S(1)} custom-call(s32[25]{0:T(128)S(1)} %dynamic-slice_bitcast_fusion.s, bf16[192,1024]{1,0:T(8,128)(2,1)S(1)} %copy-done.5, bf16[1024,8192]{1,0:T(8,128)(2,1)} %w_ref.7), custom_call_target="tpu_custom_call" | custom-call | tf_op jit(solution)/shard_map/project/pallas_call | solution.py:42
  10.5 0.8 collective-permute-start.1
  11.3 3.4 %project.3.refs_0_ = bf16[1,192,2048]{2,1,0:T(8,128)(2,1)S(1)} custom-call(s32[25]{0:T(128)S(1)} %dynamic-slice_bitcast_fusion.s, bf16[192,1024]{1,0:T(8,128)(2,1)S(1)} %copy-done.5, bf16[1024,8192]{1,0:T(8,128)(2,1)} %w_ref.7), custom_call_target="tpu_custom_call" | custom-call | tf_op jit(solution)/shard_map/project/pallas_call | solution.py:42
  14.8 2.3 %collective-permute-done.refs_1_ = bf16[1,192,2048]{2,1,0:T(8,128)(2,1)S(1)} collective-permute-done((bf16[1,192,2048]{2,1,0:T(8,128)(2,1)S(1)}, bf16[1,192,2048]{2,1,0:T(8,128)(2,1)S(1)}, u32[]{:S(2)}, u32[]{:S(2)}) %collective-permute-start) | collective-permute-done | bytes 786464 | tf_op jit(solution)/shard_map/ppermute | solution.py:303
  17.1 0.4 add_up.4.base_ref
  17.5 0.7 collective-permute-start.2
  18.2 1.8 prepare.1.refs_0_
  20.0 0.4 add_up.5
  20.4 1.3 collective-permute-start.3
  21.7 21.7 %collective-permute-done.3.refs_1_ = bf16[192,2048]{1,0:T(8,128)(2,1)S(1)} collective-permute-done((bf16[192,2048]{1,0:T(8,128)(2,1)S(1)}, bf16[192,2048]{1,0:T(8,128)(2,1)S(1)}, u32[]{:S(2)}, u32[]{:S(2)}) %collective-permute-start.3) | collective-permute-done | bytes 786464 | tf_op jit(solution)/shard_map/ppermute | solution.py:373
  43.4 0.4 add_up.6
  43.8 1.9 collective-permute-start.4
  45.8 11.1 %collective-permute-done.4.refs_1_ = bf16[192,2048]{1,0:T(8,128)(2,1)S(1)} collective-permute-done((bf16[192,2048]{1,0:T(8,128)(2,1)S(1)}, bf16[192,2048]{1,0:T(8,128)(2,1)S(1)}, u32[]{:S(2)}, u32[]{:S(2)}) %collective-permute-start.4) | collective-permute-done | bytes 786464 | tf_op jit(solution)/shard_map/ppermute | solution.py:373
  57.3 3.2 %collective-permute-start.5 = (bf16[192,2048]{1,0:T(8,128)(2,1)S(1)}, bf16[192,2048]{1,0:T(8,128)(2,1)S(1)}, u32[]{:S(2)}, u32[]{:S(2)}) collective-permute-start(bf16[192,2048]{1,0:T(8,128)(2,1)S(1)} %add_up.7.mine_ref), channel_id=1, source_target_pairs={{0,1},{1,0},{2,3},{3,2},{4,5},{5,4},{6,7},{7,6},{8,9},{9,8},{10,11... | collective-permute-start | bytes 2359304 | tf_op jit(solution)/shard_map/ppermute | solution.py:303
  60.6 2.4 %collective-permute-done.6.theirs_ref = bf16[192,1024]{1,0:T(8,128)(2,1)S(1)} collective-permute-done((bf16[192,1024]{1,0:T(8,128)(2,1)S(1)}, bf16[192,1024]{1,0:T(8,128)(2,1)S(1)}, u32[]{:S(2)}, u32[]{:S(2)}) %collective-permute-start.6) | collective-permute-done | bytes 393248 | tf_op jit(solution)/shard_map/ppermute | solution.py:303
  63.0 0.6 pair.2.residual_ref
  63.6 1.6 finish_stream.1
  65.2 1.9 collective-permute-start.7
  67.1 11.1 %collective-permute-done.7.refs_0_ = bf16[192,2048]{1,0:T(8,128)(2,1)S(1)} collective-permute-done((bf16[192,2048]{1,0:T(8,128)(2,1)S(1)}, bf16[192,2048]{1,0:T(8,128)(2,1)S(1)}, u32[]{:S(2)}, u32[]{:S(2)}) %collective-permute-start.7) | collective-permute-done | bytes 786464 | tf_op jit(solution)/shard_map/ppermute | solution.py:406
  78.2 1.9 collective-permute-start.8
  80.1 10.8 %collective-permute-done.8.refs_0_ = bf16[192,2048]{1,0:T(8,128)(2,1)S(1)} collective-permute-done((bf16[192,2048]{1,0:T(8,128)(2,1)S(1)}, bf16[192,2048]{1,0:T(8,128)(2,1)S(1)}, u32[]{:S(2)}, u32[]{:S(2)}) %collective-permute-start.8) | collective-permute-done | bytes 786464 | tf_op jit(solution)/shard_map/ppermute | solution.py:406
  90.9 2.0 collective-permute-start.9
  92.9 2.1 collective-permute-start.16
  95.0 1.3 collective-permute-start.19
  96.3 2.1 collective-permute-start.13
  98.5 3.2 %collective-permute-done.9.refs_0_ = bf16[192,2048]{1,0:T(8,128)(2,1)S(1)} collective-permute-done((bf16[192,2048]{1,0:T(8,128)(2,1)S(1)}, bf16[192,2048]{1,0:T(8,128)(2,1)S(1)}, u32[]{:S(2)}, u32[]{:S(2)}) %collective-permute-start.9) | collective-permute-done | bytes 786464 | tf_op jit(solution)/shard_map/ppermute | solution.py:406
  101.8 0.7 collective-permute-start.10
  102.5 19.1 %collective-permute-done.19.mine_ref = bf16[192,1024]{1,0:T(8,128)(2,1)S(1)} collective-permute-done((bf16[192,1024]{1,0:T(8,128)(2,1)}, bf16[192,1024]{1,0:T(8,128)(2,1)S(1)}, u32[]{:S(2)}, u32[]{:S(2)}) %collective-permute-start.19) | collective-permute-done | bytes 393248 | tf_op jit(solution)/shard_map/ppermute | solution.py:391
  121.6 0.5 collective-permute-start.18
  122.1 1.2 collective-permute-done.20.theirs_ref
  123.5 6.6 %collective-permute-done.13.refs_1_ = bf16[192,2048]{1,0:T(8,128)(2,1)S(1)} collective-permute-done((bf16[192,2048]{1,0:T(8,128)(2,1)S(1)}, bf16[192,2048]{1,0:T(8,128)(2,1)S(1)}, u32[]{:S(2)}, u32[]{:S(2)}) %collective-permute-start.13) | collective-permute-done | bytes 786464 | tf_op jit(solution)/shard_map/ppermute | solution.py:391
  130.0 0.5 collective-permute-start.11
  130.6 4.5 %split_weight.4.refs_0_ = bf16[2,8192,1024]{2,1,0:T(8,128)(2,1)S(1)} custom-call(bf16[8192,2,1024]{2,1,0:T(2,128)(2,1)} %w_ref.11), custom_call_target="tpu_custom_call" | custom-call | tf_op jit(solution)/shard_map/split_weight/pallas_call | solution.py:181
  135.2 4.5 %split_weight.5.refs_0_ = bf16[2,8192,1024]{2,1,0:T(8,128)(2,1)S(1)} custom-call(bf16[8192,2,1024]{2,1,0:T(2,128)(2,1)} %w_ref.11, bf16[2,8192,1024]{2,1,0:T(8,128)(2,1)S(1)} %split_weight.4.refs_0_), custom_call_target="tpu_custom_call", output_to_operand_aliasing={{}: (1, {})} | custom-call | tf_op jit(solution)/shard_map/split_weight/pallas_call | solution.py:181
  139.7 4.5 %split_weight.6.refs_0_ = bf16[2,8192,1024]{2,1,0:T(8,128)(2,1)S(1)} custom-call(bf16[8192,2,1024]{2,1,0:T(2,128)(2,1)} %w_ref.11, bf16[2,8192,1024]{2,1,0:T(8,128)(2,1)S(1)} %split_weight.5.refs_0_), custom_call_target="tpu_custom_call", output_to_operand_aliasing={{}: (1, {})} | custom-call | tf_op jit(solution)/shard_map/split_weight/pallas_call | solution.py:181
  144.2 4.5 %split_weight.7.refs_3_ = bf16[2,8192,1024]{2,1,0:T(8,128)(2,1)S(1)} custom-call(bf16[8192,2,1024]{2,1,0:T(2,128)(2,1)} %w_ref.11, bf16[2,8192,1024]{2,1,0:T(8,128)(2,1)S(1)} %split_weight.6.refs_0_), custom_call_target="tpu_custom_call", output_to_operand_aliasing={{}: (1, {})} | custom-call | tf_op jit(solution)/shard_map/split_weight/pallas_call | solution.py:181
  148.8 11.1 %copy-done = bf16[2,8192,1024]{2,1,0:T(8,128)(2,1)} copy-done((bf16[2,8192,1024]{2,1,0:T(8,128)(2,1)}, bf16[2,8192,1024]{2,1,0:T(8,128)(2,1)S(1)}, u32[]{:S(2)}) %copy-start) | copy-done | bytes 33554456
  159.8 0.8 pair.3.refs_1_
  160.6 10.5 %copy-done.1 = bf16[2,8192,1024]{2,1,0:T(8,128)(2,1)S(1)} copy-done((bf16[2,8192,1024]{2,1,0:T(8,128)(2,1)S(1)}, bf16[2,8192,1024]{2,1,0:T(8,128)(2,1)}, u32[]{:S(2)}) %copy-start.1) | copy-done | bytes 33554456
  171.2 4.5 %gate_products.4 = (f32[2,384,1024]{2,1,0:T(8,128)S(1)}, f32[384,1]{1,0:T(8,128)S(1)}, bf16[2,8192,1024]{2,1,0:T(8,128)(2,1)S(1)}) custom-call(s32[25]{0:T(128)S(1)} %dynamic-slice_bitcast_fusion.s, bf16[192,2048]{1,0:T(8,128)(2,1)S(1)} %get-tuple-element.14.refs_0_, bf16[192,2048]{1,0:T(8,128)(2,1)S(1)} %pair.3.refs_1_, ...), custom_call_target="tpu_custom_call", output_to_operand_aliasing={{2}: (4, {})} | custom-call | tf_op jit(solution)/shard_map/gate_products/pallas_call | solution.py:290
  175.7 11.1 %copy-done.2 = bf16[2,8192,1024]{2,1,0:T(8,128)(2,1)} copy-done((bf16[2,8192,1024]{2,1,0:T(8,128)(2,1)}, bf16[2,8192,1024]{2,1,0:T(8,128)(2,1)S(1)}, u32[]{:S(2)}) %copy-start.2) | copy-done | bytes 33554456
  186.8 1.6 copy-done.4
  188.4 10.5 %copy-done.3 = bf16[2,8192,1024]{2,1,0:T(8,128)(2,1)S(1)} copy-done((bf16[2,8192,1024]{2,1,0:T(8,128)(2,1)S(1)}, bf16[2,8192,1024]{2,1,0:T(8,128)(2,1)}, u32[]{:S(2)}) %copy-start.3) | copy-done | bytes 33554456
  199.0 11.9 %gate_products.5 = (f32[2,384,1024]{2,1,0:T(8,128)}, f32[384,1]{1,0:T(8,128)S(1)}, bf16[2,8192,1024]{2,1,0:T(8,128)(2,1)S(1)}) custom-call(s32[25]{0:T(128)S(1)} %dynamic-slice_bitcast_fusion.s, bf16[192,2048]{1,0:T(8,128)(2,1)S(1)} %collective-permute-done.7.refs_0_, ...), custom_call_target="tpu_custom_call", output_to_operand_aliasing={{2}: (6, {}), {0}: (7, {}), {1}: (8, {})} | custom-call | tf_op jit(solution)/shard_map/gate_products/pallas_call | solution.py:290
  210.9 8.3 %gate_products.6 = (f32[2,384,1024]{2,1,0:T(8,128)}, f32[384,1]{1,0:T(8,128)S(1)}, bf16[2,8192,1024]{2,1,0:T(8,128)(2,1)S(1)}) custom-call(s32[25]{0:T(128)S(1)} %dynamic-slice_bitcast_fusion.s, bf16[192,2048]{1,0:T(8,128)(2,1)S(1)} %collective-permute-done.8.refs_0_, ...), custom_call_target="tpu_custom_call", output_to_operand_aliasing={{2}: (6, {}), {0}: (7, {}), {1}: (8, {})} | custom-call | tf_op jit(solution)/shard_map/gate_products/pallas_call | solution.py:290
  219.3 4.7 %gate_products.7 = bf16[384,1024]{1,0:T(8,128)(2,1)} custom-call(s32[25]{0:T(128)S(1)} %dynamic-slice_bitcast_fusion.s, bf16[192,2048]{1,0:T(8,128)(2,1)S(1)} %collective-permute-done.9.refs_0_, bf16[192,2048]{1,0:T(8,128)(2,1)S(1)} %collective-permute-done.10.refs_1_, bf16[192,2048]{1,0:T(8,128)(2,1)S(1)} %collective-permute-done.11.refs_2_, ...), custom_call_target="tpu_custom_call" | custom-call | tf_op jit(solution)/shard_map/gate_products/pallas_call | solution.py:290
  (30 shorter events, 0.9 us)
Async XLA Ops:
  0.6 130.0 %copy-start.7 = (bf16[8192]{0:T(1024)(128)(2,1)S(1)}, bf16[8192]{0:T(1024)(128)(2,1)}, u32[]{:S(2)}) copy-start(bf16[8192]{0:T(1024)(128)(2,1)} %param.9) | copy-start | bytes 49156
  1.3 1.0 copy-start.5
  2.3 58.2 %copy-start.6 = (bf16[192,1024]{1,0:T(8,128)(2,1)S(1)}, bf16[192,1024]{1,0:T(8,128)(2,1)}, u32[]{:S(2)}) copy-start(bf16[192,1024]{1,0:T(8,128)(2,1)} %mine_ref.1) | copy-start | bytes 1179652
  10.5 7.7 %collective-permute-start.1 = (bf16[3,192,2048]{2,1,0:T(8,128)(2,1)S(1)}, bf16[3,192,2048]{2,1,0:T(8,128)(2,1)S(1)}, u32[]{:S(2)}, u32[]{:S(2)}) collective-permute-start(bf16[3,192,2048]{2,1,0:T(8,128)(2,1)S(1)} %project.2.mine_ref.refs_0_), channel_id=1, source_target_pairs={{0,1},{1,0},{2,3},{3,2},{4,5},{5,4},{6,7},{7,6},{8,9},{9,8},{10,11... | collective-permute-start | bytes 7077896 | tf_op jit(solution)/shard_map/ppermute | solution.py:303
  14.7 2.4 %collective-permute-start = (bf16[1,192,2048]{2,1,0:T(8,128)(2,1)S(1)}, bf16[1,192,2048]{2,1,0:T(8,128)(2,1)S(1)}, u32[]{:S(2)}, u32[]{:S(2)}) collective-permute-start(bf16[1,192,2048]{2,1,0:T(8,128)(2,1)S(1)} %project.3.refs_0_), channel_id=1, source_target_pairs={{0,1},{1,0},{2,3},{3,2},{4,5},{5,4},{6,7},{7,6},{8,9},{9,8},{10,11... | collective-permute-start | bytes 2359304 | tf_op jit(solution)/shard_map/ppermute | solution.py:303
  17.5 2.5 %collective-permute-start.2 = (bf16[192,2048]{1,0:T(8,128)(2,1)S(1)}, bf16[192,2048]{1,0:T(8,128)(2,1)S(1)}, u32[]{:S(2)}, u32[]{:S(2)}) collective-permute-start(bf16[192,2048]{1,0:T(8,128)(2,1)S(1)} %add_up.4.base_ref), channel_id=1, source_target_pairs={{0,4},{13,9},{2,6},{15,11},{16,20},{29,25},{18,22},{31,27}} | collective-permute-start | bytes 2359304 | tf_op jit(solution)/shard_map/ppermute | solution.py:373
  20.4 23.0 %collective-permute-start.3 = (bf16[192,2048]{1,0:T(8,128)(2,1)S(1)}, bf16[192,2048]{1,0:T(8,128)(2,1)S(1)}, u32[]{:S(2)}, u32[]{:S(2)}) collective-permute-start(bf16[192,2048]{1,0:T(8,128)(2,1)S(1)} %add_up.5), channel_id=1, source_target_pairs={{0,4},{4,8},{9,5},{13,9},{2,6},{6,10},{11,7},{15,11},{16,20},{20,2... | collective-permute-start | bytes 2359304 | tf_op jit(solution)/shard_map/ppermute | solution.py:373
  43.8 13.0 %collective-permute-start.4 = (bf16[192,2048]{1,0:T(8,128)(2,1)S(1)}, bf16[192,2048]{1,0:T(8,128)(2,1)S(1)}, u32[]{:S(2)}, u32[]{:S(2)}) collective-permute-start(bf16[192,2048]{1,0:T(8,128)(2,1)S(1)} %add_up.6), channel_id=1, source_target_pairs={{0,4},{4,8},{8,12},{5,1},{9,5},{13,9},{2,6},{6,10},{10,14},{7,3},{... | collective-permute-start | bytes 2359304 | tf_op jit(solution)/shard_map/ppermute | solution.py:373
  57.3 6.3 %collective-permute-start.5 = (bf16[192,2048]{1,0:T(8,128)(2,1)S(1)}, bf16[192,2048]{1,0:T(8,128)(2,1)S(1)}, u32[]{:S(2)}, u32[]{:S(2)}) collective-permute-start(bf16[192,2048]{1,0:T(8,128)(2,1)S(1)} %add_up.7.mine_ref), channel_id=1, source_target_pairs={{0,1},{1,0},{2,3},{3,2},{4,5},{5,4},{6,7},{7,6},{8,9},{9,8},{10,11... | collective-permute-start | bytes 2359304 | tf_op jit(solution)/shard_map/ppermute | solution.py:303
  60.5 2.5 %collective-permute-start.6 = (bf16[192,1024]{1,0:T(8,128)(2,1)S(1)}, bf16[192,1024]{1,0:T(8,128)(2,1)S(1)}, u32[]{:S(2)}, u32[]{:S(2)}) collective-permute-start(bf16[192,1024]{1,0:T(8,128)(2,1)S(1)} %copy-done.6), channel_id=1, source_target_pairs={{0,1},{1,0},{2,3},{3,2},{4,5},{5,4},{6,7},{7,6},{8,9},{9,8},{10,11... | collective-permute-start | bytes 1179656 | tf_op jit(solution)/shard_map/ppermute | solution.py:303
  65.2 13.0 %collective-permute-start.7 = (bf16[192,2048]{1,0:T(8,128)(2,1)S(1)}, bf16[192,2048]{1,0:T(8,128)(2,1)S(1)}, u32[]{:S(2)}, u32[]{:S(2)}) collective-permute-start(bf16[192,2048]{1,0:T(8,128)(2,1)S(1)} %get-tuple-element.14.refs_0_), channel_id=1, source_target_pairs={{0,4},{4,8},{8,12},{5,1},{9,5},{13,9},{2,6},{6,10},{10,14},{7,3},{... | collective-permute-start | bytes 2359304 | tf_op jit(solution)/shard_map/ppermute | solution.py:406
  78.2 12.7 %collective-permute-start.8 = (bf16[192,2048]{1,0:T(8,128)(2,1)S(1)}, bf16[192,2048]{1,0:T(8,128)(2,1)S(1)}, u32[]{:S(2)}, u32[]{:S(2)}) collective-permute-start(bf16[192,2048]{1,0:T(8,128)(2,1)S(1)} %collective-permute-done.7.refs_0_), channel_id=1, source_target_pairs={{4,8},{8,12},{5,1},{9,5},{6,10},{10,14},{7,3},{11,7},{20,24},{24,2... | collective-permute-start | bytes 2359304 | tf_op jit(solution)/shard_map/ppermute | solution.py:406
  90.9 10.8 %collective-permute-start.9 = (bf16[192,2048]{1,0:T(8,128)(2,1)S(1)}, bf16[192,2048]{1,0:T(8,128)(2,1)S(1)}, u32[]{:S(2)}, u32[]{:S(2)}) collective-permute-start(bf16[192,2048]{1,0:T(8,128)(2,1)S(1)} %collective-permute-done.8.refs_0_), channel_id=1, source_target_pairs={{8,12},{5,1},{10,14},{7,3},{24,28},{21,17},{26,30},{23,19}} | collective-permute-start | bytes 2359304 | tf_op jit(solution)/shard_map/ppermute | solution.py:406
  92.9 28.7 %collective-permute-start.16 = (bf16[192,2048]{1,0:T(8,128)(2,1)S(1)}, bf16[192,2048]{1,0:T(8,128)(2,1)S(1)}, u32[]{:S(2)}, u32[]{:S(2)}) collective-permute-start(bf16[192,2048]{1,0:T(8,128)(2,1)S(1)} %collective-permute-done.7.refs_0_), channel_id=1, source_target_pairs={{4,6},{6,4},{8,10},{10,8},{12,14},{14,12},{1,3},{3,1},{5,7},{7,5},... | collective-permute-start | bytes 2359304 | tf_op jit(solution)/shard_map/ppermute | solution.py:391
  95.0 26.6 %collective-permute-start.19 = (bf16[192,1024]{1,0:T(8,128)(2,1)}, bf16[192,1024]{1,0:T(8,128)(2,1)S(1)}, u32[]{:S(2)}, u32[]{:S(2)}) collective-permute-start(bf16[192,1024]{1,0:T(8,128)(2,1)} %get-tuple-element.11), channel_id=1, source_target_pairs={{0,2},{2,0},{1,3},{3,1},{4,6},{6,4},{5,7},{7,5},{8,10},{10,8},{9,1... | collective-permute-start | bytes 1179656 | tf_op jit(solution)/shard_map/ppermute | solution.py:391
  96.3 33.7 %collective-permute-start.13 = (bf16[192,2048]{1,0:T(8,128)(2,1)S(1)}, bf16[192,2048]{1,0:T(8,128)(2,1)S(1)}, u32[]{:S(2)}, u32[]{:S(2)}) collective-permute-start(bf16[192,2048]{1,0:T(8,128)(2,1)S(1)} %collective-permute-done.8.refs_0_), channel_id=1, source_target_pairs={{8,10},{10,8},{12,14},{14,12},{1,3},{3,1},{5,7},{7,5},{24,26},{26,... | collective-permute-start | bytes 2359304 | tf_op jit(solution)/shard_map/ppermute | solution.py:391
  98.5 31.6 %collective-permute-start.17 = (bf16[192,2048]{1,0:T(8,128)(2,1)S(1)}, bf16[192,2048]{1,0:T(8,128)(2,1)S(1)}, u32[]{:S(2)}, u32[]{:S(2)}) collective-permute-start(bf16[192,2048]{1,0:T(8,128)(2,1)S(1)} %collective-permute-done.7.refs_0_), channel_id=1, source_target_pairs={{0,1},{1,0},{2,3},{3,2},{4,5},{5,4},{6,7},{7,6},{8,9},{9,8},{10,11... | collective-permute-start | bytes 2359304 | tf_op jit(solution)/shard_map/ppermute | solution.py:303
  101.8 28.8 %collective-permute-start.10 = (bf16[192,2048]{1,0:T(8,128)(2,1)S(1)}, bf16[192,2048]{1,0:T(8,128)(2,1)S(1)}, u32[]{:S(2)}, u32[]{:S(2)}) collective-permute-start(bf16[192,2048]{1,0:T(8,128)(2,1)S(1)} %collective-permute-done.9.refs_0_), channel_id=1, source_target_pairs={{12,14},{14,12},{1,3},{3,1},{28,30},{30,28},{17,19},{19,17}} | collective-permute-start | bytes 2359304 | tf_op jit(solution)/shard_map/ppermute | solution.py:391
  121.6 1.7 collective-permute-start.20
  121.6 66.8 %collective-permute-start.18 = (bf16[192,2048]{1,0:T(8,128)(2,1)S(1)}, bf16[192,2048]{1,0:T(8,128)(2,1)S(1)}, u32[]{:S(2)}, u32[]{:S(2)}) collective-permute-start(bf16[192,2048]{1,0:T(8,128)(2,1)S(1)} %collective-permute-done.16.refs_1_), channel_id=1, source_target_pairs={{0,1},{1,0},{2,3},{3,2},{4,5},{5,4},{6,7},{7,6},{8,9},{9,8},{10,11... | collective-permute-start | bytes 2359304 | tf_op jit(solution)/shard_map/ppermute | solution.py:303
  123.3 87.6 %collective-permute-start.14 = (bf16[192,2048]{1,0:T(8,128)(2,1)S(1)}, bf16[192,2048]{1,0:T(8,128)(2,1)S(1)}, u32[]{:S(2)}, u32[]{:S(2)}) collective-permute-start(bf16[192,2048]{1,0:T(8,128)(2,1)S(1)} %collective-permute-done.8.refs_0_), channel_id=1, source_target_pairs={{0,1},{1,0},{2,3},{3,2},{4,5},{5,4},{6,7},{7,6},{8,9},{9,8},{10,11... | collective-permute-start | bytes 2359304 | tf_op jit(solution)/shard_map/ppermute | solution.py:303
  130.0 80.9 %collective-permute-start.15 = (bf16[192,2048]{1,0:T(8,128)(2,1)S(1)}, bf16[192,2048]{1,0:T(8,128)(2,1)S(1)}, u32[]{:S(2)}, u32[]{:S(2)}) collective-permute-start(bf16[192,2048]{1,0:T(8,128)(2,1)S(1)} %collective-permute-done.13.refs_1_), channel_id=1, source_target_pairs={{0,1},{1,0},{2,3},{3,2},{4,5},{5,4},{6,7},{7,6},{8,9},{9,8},{10,11... | collective-permute-start | bytes 2359304 | tf_op jit(solution)/shard_map/ppermute | solution.py:303
  130.0 89.2 %collective-permute-start.11 = (bf16[192,2048]{1,0:T(8,128)(2,1)S(1)}, bf16[192,2048]{1,0:T(8,128)(2,1)S(1)}, u32[]{:S(2)}, u32[]{:S(2)}) collective-permute-start(bf16[192,2048]{1,0:T(8,128)(2,1)S(1)} %collective-permute-done.9.refs_0_), channel_id=1, source_target_pairs={{0,1},{1,0},{2,3},{3,2},{4,5},{5,4},{6,7},{7,6},{8,9},{9,8},{10,11... | collective-permute-start | bytes 2359304 | tf_op jit(solution)/shard_map/ppermute | solution.py:303
  130.5 88.7 %collective-permute-start.12 = (bf16[192,2048]{1,0:T(8,128)(2,1)S(1)}, bf16[192,2048]{1,0:T(8,128)(2,1)S(1)}, u32[]{:S(2)}, u32[]{:S(2)}) collective-permute-start(bf16[192,2048]{1,0:T(8,128)(2,1)S(1)} %collective-permute-done.10.refs_1_), channel_id=1, source_target_pairs={{0,1},{1,0},{2,3},{3,2},{4,5},{5,4},{6,7},{7,6},{8,9},{9,8},{10,11... | collective-permute-start | bytes 2359304 | tf_op jit(solution)/shard_map/ppermute | solution.py:303
  148.8 11.1 %copy-start = (bf16[2,8192,1024]{2,1,0:T(8,128)(2,1)}, bf16[2,8192,1024]{2,1,0:T(8,128)(2,1)S(1)}, u32[]{:S(2)}) copy-start(bf16[2,8192,1024]{2,1,0:T(8,128)(2,1)S(1)} %split_weight.7.refs_3_) | copy-start | bytes 100663296
  160.6 10.5 %copy-start.1 = (bf16[2,8192,1024]{2,1,0:T(8,128)(2,1)S(1)}, bf16[2,8192,1024]{2,1,0:T(8,128)(2,1)}, u32[]{:S(2)}) copy-start(bf16[2,8192,1024]{2,1,0:T(8,128)(2,1)} %copy-done) | copy-start | bytes 100663296
  175.7 11.1 %copy-start.2 = (bf16[2,8192,1024]{2,1,0:T(8,128)(2,1)}, bf16[2,8192,1024]{2,1,0:T(8,128)(2,1)S(1)}, u32[]{:S(2)}) copy-start(bf16[2,8192,1024]{2,1,0:T(8,128)(2,1)S(1)} %get-tuple-element.15.refs_5_) | copy-start | bytes 100663296
  186.8 1.6 copy-start.4
  188.4 10.5 %copy-start.3 = (bf16[2,8192,1024]{2,1,0:T(8,128)(2,1)S(1)}, bf16[2,8192,1024]{2,1,0:T(8,128)(2,1)}, u32[]{:S(2)}) copy-start(bf16[2,8192,1024]{2,1,0:T(8,128)(2,1)} %copy-done.2) | copy-start | bytes 100663296
